TPU v7x, 8 devices: a whole 2x2x1 slice. The times are simulated.
8 devices in a mesh: dp: 2 (over y, z), ep: 4 (over x, core).
Axes of the slice: x: 2, y: 2, z: 1, core: 2. Of those that a mesh axis runs over, the one named last changes fastest.
Arguments:
- x: bfloat16 [2, 4, 256, 7168], P('dp', 'ep'), parts along dimension 0
- expert: int32 [2, 4, 256, 8], P('dp', 'ep'), parts along dimension 0
- slot: int32 [2, 4, 256, 8], P('dp', 'ep'), parts along dimension 0
- gate: float32 [2, 4, 256, 8], P('dp', 'ep'), parts along dimension 0
- w_gate: bfloat16 [24, 7168, 2048], P('ep')
- w_up: bfloat16 [24, 7168, 2048], P('ep')
- w_down: bfloat16 [24, 2048, 7168], P('ep')
- s_gate: bfloat16 [7168, 2048], replicated
- s_up: bfloat16 [7168, 2048], replicated
- s_down: bfloat16 [2048, 7168], replicated
Outputs:
- y: bfloat16 [2, 4, 256, 7168], P('dp', 'ep'), parts along dimension 0
There are 2 independent parts. A program takes and returns all parts, laid end to end along the dimension named above; an argument that names none is the same for every part.
All inputs are finite; a program needn't handle non-finite values.
Results may differ from a plain program's by a relative error of at most 0.009.
Values are sent between devices in bfloat16 or wider.
A program may use at most 2 GiB of HBM per device.

v0:
```python
import jax
import jax.numpy as jnp
from jax import lax
from jax.sharding import NamedSharding, PartitionSpec as P


def einsum(form, a, b):
    return jnp.einsum(form, a.astype(jnp.float32), b.astype(jnp.float32))


def for_all(x, s_gate, s_up, s_down):
    h = jax.nn.silu(einsum("...d,df->...f", x, s_gate)) * einsum("...d,df->...f", x, s_up)
    return einsum("...f,fd->...d", h.astype(jnp.bfloat16), s_down)


def solution(mesh):
    def placed(v, *spec):
        return lax.with_sharding_constraint(v, NamedSharding(mesh, P(*spec)))

    def step(x, expert, slot, gate, w_gate, w_up, w_down, s_gate, s_up, s_down):
        experts, (tokens, top) = w_gate.shape[0], expert.shape[2:]
        slots = 5 * tokens * top // (4 * experts)
        to_expert = jax.nn.one_hot(expert, experts, dtype=jnp.bfloat16)
        to_slot = jax.nn.one_hot(slot, slots, dtype=jnp.bfloat16)
        weighted = to_expert * gate[..., None].astype(jnp.bfloat16)
        dispatch = einsum("abtke,abtkc->abtec", to_expert, to_slot).astype(jnp.bfloat16)
        combine = einsum("abtke,abtkc->abtec", weighted, to_slot).astype(jnp.bfloat16)
        z = einsum("abtec,abtd->aebcd", dispatch, x).astype(jnp.bfloat16)
        z = placed(z, "dp", None, "ep", None, None)
        z = placed(z, "dp", "ep", None, None, None)
        h = jax.nn.silu(einsum("aebcd,edf->aebcf", z, w_gate))
        h = (h * einsum("aebcd,edf->aebcf", z, w_up)).astype(jnp.bfloat16)
        out = einsum("aebcf,efd->aebcd", h, w_down).astype(jnp.bfloat16)
        out = placed(out, "dp", "ep", None, None, None)
        out = placed(out, "dp", None, "ep", None, None)
        y = einsum("abtec,aebcd->abtd", combine, out)
        return (y + for_all(x, s_gate, s_up, s_down)).astype(jnp.bfloat16)

    return step
```

profile of v0, /device:TPU:0, one launch (start us, length us, event | category | flops | bytes accessed | tf_op | source)
XLA Modules:
  0.0 1237.0 jit_solution(17576896323212111197)
XLA Ops:
  0.0 0.8 copy.11
  0.8 0.0 copy-start.1
  0.8 0.8 copy.9
  1.7 0.0 copy-start.3
  1.7 2.8 convolution_convert_fusion.1
  4.5 18.5 %convolution_convert_fusion = bf16[24,106,7168]{2,1,0:T(8,128)(2,1)} fusion(bf16[1,1,256,7168]{3,2,1,0:T(8,128)(2,1)} %param.3, bf16[256,24,106]{2,1,0:T(8,128)(2,1)S(1)} %convolution_convert_fusion.1), kind=kOutput, calls=%fused_computation.11 | convolution fusion | flops 9354756096 | bytes 41443328 | tf_op jit(solution)/abtec,abtd->aebcd/dot_general | solution.py:8
  23.0 0.0 copy-done.1
  23.0 0.0 copy-done.3
  23.0 437.3 %all-to-all.4 = bf16[1,4,6,1,106,7168]{5,4,2,3,0,1:T(8,128)(2,1)} all-to-all(bf16[1,4,6,1,106,7168]{5,4,2,3,0,1:T(8,128)(2,1)} %bitcast.110), channel_id=1, replica_groups=mesh['dp'=2,'ep'=4] {'ep'}, dimensions={1} | all-to-all | bytes 72941568 | tf_op jit(solution)/sharding_constraint;jit(solution)/sharding_constraint | solution.py:18
  460.3 95.3 %fusion.2 = f32[6,4,106,2048]{3,2,1,0:T(8,128)} fusion(bf16[6,7168,2048]{2,1,0:T(8,128)(2,1)} %param.5, bf16[1,4,6,1,106,7168]{5,4,2,3,0,1:T(8,128)(2,1)} %all-to-all.4), kind=kOutput, calls=%fused_computation.2 | convolution fusion | flops 74692165632 | bytes 233472000 | tf_op jit(solution)/aebcd,edf->aebcf/dot_general | solution.py:8
  555.6 97.1 %fusion.12 = bf16[1,6,4,106,2048]{4,3,2,1,0:T(8,128)(2,1)} fusion(f32[6,4,106,2048]{3,2,1,0:T(8,128)} %fusion.2, bf16[6,7168,2048]{2,1,0:T(8,128)(2,1)} %param.4, bf16[1,4,6,1,106,7168]{5,4,2,3,0,1:T(8,128)(2,1)} %all-to-all.4), kind=kOutput, calls=%fused_computation.13 | convolution fusion | flops 74723426304 | bytes 243892224 | tf_op jit(solution)/aebcd,edf->aebcf/dot_general | solution.py:8
  652.7 91.1 %convert_bitcast_fusion = bf16[1,6,4,1,106,7168]{5,4,2,1,3,0:T(8,128)(2,1)} fusion(bf16[6,2048,7168]{2,1,0:T(8,128)(2,1)} %param.6, bf16[1,6,4,106,2048]{4,3,2,1,0:T(8,128)(2,1)} %fusion.12), kind=kOutput, calls=%fused_computation.8 | convolution fusion | flops 74710401024 | bytes 223051776 | tf_op jit(solution)/aebcf,efd->aebcd/dot_general | solution.py:8
  743.8 26.5 %copy.15 = bf16[1,6,4,1,106,7168]{5,4,1,3,0,2:T(8,128)(2,1)} copy(bf16[1,6,4,1,106,7168]{5,4,2,1,3,0:T(8,128)(2,1)} %convert_bitcast_fusion) | data formatting | bytes 72941568 | tf_op jit(solution)/sharding_constraint;jit(solution)/sharding_constraint | solution.py:18
  770.2 0.0 copy-start.4
  770.2 10.8 all-to-all-start.1
  781.0 0.0 copy-done.5
  781.1 0.1 copy.10
  781.2 2.9 convolution_convert_fusion.2
  784.1 14.5 %fusion.34 = f32[1,1,256,2048]{3,2,1,0:T(8,128)S(1)} fusion(bf16[7168,2048]{1,0:T(8,128)(2,1)} %param.7, bf16[1,1,256,7168]{3,2,1,0:T(8,128)(2,1)} %param.3), kind=kOutput, calls=%fused_computation.31 | convolution fusion | flops 7516192768 | bytes 35127296 | tf_op jit(solution)/...d,df->...f/dot_general | solution.py:8
  798.6 0.0 copy-done
  798.6 13.9 %fusion.40 = bf16[256,2048]{1,0:T(8,128)(2,1)S(1)} fusion(bf16[7168,2048]{1,0:T(8,128)(2,1)} %param.8, bf16[1,1,256,7168]{3,2,1,0:T(8,128)(2,1)S(1)} %copy-done, f32[1,1,256,2048]{3,2,1,0:T(8,128)S(1)} %fusion.34), kind=kOutput, calls=%fused_computation.33 | convolution fusion | flops 7519338496 | bytes 36175872 | tf_op jit(solution)/...d,df->...f/dot_general | solution.py:8
  812.6 384.3 %all-to-all-done.1 = bf16[1,6,4,1,106,7168]{5,4,1,3,0,2:T(8,128)(2,1)} async-done(((bf16[1,6,4,1,106,7168]{5,4,1,3,0,2:T(8,128)(2,1)}), bf16[1,6,4,1,106,7168]{5,4,1,3,0,2:T(8,128)(2,1)}, u32[]{:S(2)}, u32[]{:S(2)}) %all-to-all-start.1) | async-done | bytes 36470816 | tf_op jit(solution)/sharding_constraint;jit(solution)/sharding_constraint | solution.py:18
  1196.9 20.4 %convolution_bitcast_fusion = f32[256,7168]{1,0:T(8,128)} fusion(bf16[24,106,7168]{2,1,0:T(8,128)(2,1)} %bitcast.24, bf16[256,24,106]{2,1,0:T(8,128)(2,1)S(1)} %convolution_convert_fusion.2), kind=kOutput, calls=%fused_computation.20 | convolution fusion | flops 9336520704 | bytes 45113344 | tf_op jit(solution)/abtec,aebcd->abtd/dot_general | solution.py:8
  1217.3 19.7 %fusion.22 = bf16[1,1,256,7168]{3,2,1,0:T(8,128)(2,1)} fusion(f32[256,7168]{1,0:T(8,128)} %convolution_bitcast_fusion, bf16[256,2048]{1,0:T(8,128)(2,1)S(1)} %fusion.40, bf16[2048,7168]{1,0:T(8,128)(2,1)} %param.9), kind=kOutput, calls=%fused_computation.23 | convolution fusion | flops 7519862784 | bytes 41418752 | tf_op jit(solution)/...f,fd->...d/dot_general | solution.py:8
  (6 shorter events, 0.0 us)
Async XLA Ops:
  0.8 22.2 %copy-start.1 = (s32[256,8]{1,0:T(8,128)}, s32[256,8]{1,0:T(8,128)S(1)}, u32[]{:S(2)}) copy-start(s32[256,8]{1,0:T(8,128)S(1)} %copy.11) | copy-start | bytes 24580
  1.7 21.3 %copy-start.3 = (s32[256,8]{1,0:T(8,128)}, s32[256,8]{1,0:T(8,128)S(1)}, u32[]{:S(2)}) copy-start(s32[256,8]{1,0:T(8,128)S(1)} %copy.9) | copy-start | bytes 24580
  770.2 10.8 copy-start.5
  770.2 11.0 copy-start.2
  770.2 11.0 copy-start.4
  770.2 426.6 %all-to-all-start.1 = ((bf16[1,6,4,1,106,7168]{5,4,1,3,0,2:T(8,128)(2,1)}), bf16[1,6,4,1,106,7168]{5,4,1,3,0,2:T(8,128)(2,1)}, u32[]{:S(2)}, u32[]{:S(2)}) async-start(bf16[1,6,4,1,106,7168]{5,4,1,3,0,2:T(8,128)(2,1)} %copy.15), calls=%async_computation.1 | async-start | bytes 77070336 | tf_op jit(solution)/sharding_constraint;jit(solution)/sharding_constraint | solution.py:18
  784.1 14.5 %copy-start = (bf16[1,1,256,7168]{3,2,1,0:T(8,128)(2,1)S(1)}, bf16[1,1,256,7168]{3,2,1,0:T(8,128)(2,1)}, u32[]{:S(2)}) copy-start(bf16[1,1,256,7168]{3,2,1,0:T(8,128)(2,1)} %param.3) | copy-start | bytes 11010052
where the time goes:
time: 1240 us
  blocking collectives  437 us (35%)
  waiting for transfers between devices  384 us (31%)
  matrix products  376 us (30%)
  local copies, waits for them, and re-layouts  28.3 us (2%)
    another operation x1, blocking collectives, placed(): return lax.with_sharding_constraint(v, NamedSharding(mesh, P(*spec)))  437 us
    another operation x1, waiting for transfers between devices, placed(): return lax.with_sharding_constraint(v, NamedSharding(mesh, P(*spec)))  384 us
    dot_general x10, matrix products, einsum(): return jnp.einsum(form, a.astype(jnp.float32), b.astype(jnp.float32))  376 us
    another operation x1, local copies, waits for them, and re-layouts, placed(): return lax.with_sharding_constraint(v, NamedSharding(mesh, P(*spec)))  26.5 us
  transfers between devices with their start and end apart: 1, of which 1 were waited for; matrix products, arithmetic and copies ran while one was open for 3% of the time, Pallas kernels for 0%

commit v1 on v0

v1 whole, which is shorter than its diff:
```python
import functools

import jax
import jax.numpy as jnp
from jax import lax
from jax.experimental import pallas as pl
from jax.experimental.pallas import tpu as pltpu
from jax.sharding import PartitionSpec as P

SAME = [(0, 1), (1, 0), (2, 3), (3, 2)]
CROSS = [(0, 2), (1, 3), (2, 0), (3, 1)]
STEP = 112
FIRST = 2048
CHUNKS = (1024, 3072, 3072)
VMEM = 62 * 2**20


def silu(g):
    return g / (1.0 + jnp.exp(-g))


def tables(expert, slot, gate, experts, slots):
    expert, slot, gate = expert.T, slot.T, gate.T
    hit = (expert[None] == jnp.arange(experts)[:, None, None]) & (slot < slots)[None]
    code = jnp.sum(jnp.where(hit, slot[None] + 1, 0), 1) - 1
    weight = jnp.sum(jnp.where(hit, gate[None], 0.0), 1)
    return jnp.stack([code.astype(jnp.float32), weight])


def up_kernel(depth, block, first, meta, code, x0, x1, x2, x3, wg, wu, *refs):
    if first:
        (g_out, u_out, z) = refs
    else:
        (g_in, u_in, h_out, z) = refs
    e, n = pl.program_id(0), pl.program_id(1)
    total = pl.multiple_of(meta[e * 8 + 4], 16)

    @pl.when(n == 0)
    def _():
        rows = lax.broadcasted_iota(jnp.int32, (STEP, 256), 0)
        for k, x in enumerate((x0, x1, x2, x3)):
            pick = (rows == code[0, k : k + 1, :]).astype(jnp.bfloat16)
            at = pl.multiple_of(meta[e * 8 + k], 16)

            @pl.loop(0, depth // 512)
            def _(c):
                cols = pl.ds(pl.multiple_of(c * 512, 512), 512)
                part = jnp.dot(pick, x[:, cols], preferred_element_type=jnp.float32)
                z[pl.ds(at, STEP), cols] = part.astype(jnp.bfloat16)

        z[pl.ds(total, STEP), :] = jnp.zeros((STEP, depth), jnp.bfloat16)

    size = (total + STEP - 1) // STEP
    for v in range(5):

        @pl.when(size == v)
        def _(v=v):
            m = v * STEP
            if v:
                g = jnp.dot(z[:m, :], wg[0], preferred_element_type=jnp.float32)
                u = jnp.dot(z[:m, :], wu[0], preferred_element_type=jnp.float32)
                if first:
                    g_out[0, :m, :] = g
                    u_out[0, :m, :] = u
                else:
                    g = g + g_in[0, :m, :]
                    u = u + u_in[0, :m, :]
                    h_out[0, :m, :] = (silu(g) * u).astype(jnp.bfloat16)
            if not first:
                h_out[0, m:, :] = jnp.zeros((5 * STEP - m, block), jnp.bfloat16)


def up(meta, code, xs, w_gate, w_up, start, block, partial=None):
    experts, _, ff = w_gate.shape
    depth = xs[0].shape[1]
    first = partial is None
    weight = pl.BlockSpec(
        (pl.Element(1), pl.Element(depth), pl.Element(block)),
        lambda e, n, m: (e, start, n * block),
    )
    whole = pl.BlockSpec((256, depth), lambda e, n, m: (0, 0), pipeline_mode=pl.Buffered(1))
    acc = pl.BlockSpec((1, 4 * STEP, block), lambda e, n, m: (e, 0, n))
    acc_shape = jax.ShapeDtypeStruct((experts, 4 * STEP, ff), jnp.float32)
    if first:
        out_shape, out_specs = [acc_shape] * 2, [acc] * 2
    else:
        out_shape = jax.ShapeDtypeStruct((experts, 5 * STEP, ff), jnp.bfloat16)
        out_specs = pl.BlockSpec((1, 5 * STEP, block), lambda e, n, m: (e, 0, n))
    return pl.pallas_call(
        functools.partial(up_kernel, depth, block, first),
        grid_spec=pltpu.PrefetchScalarGridSpec(
            num_scalar_prefetch=1,
            grid=(experts, ff // block),
            in_specs=[pl.BlockSpec((1, 4, 256), lambda e, n, m: (e, 0, 0))]
            + [whole] * 4
            + [weight] * 2
            + ([] if first else [acc] * 2),
            out_specs=out_specs,
            scratch_shapes=[pltpu.VMEM((5 * STEP, depth), jnp.bfloat16)],
        ),
        out_shape=out_shape,
        compiler_params=pltpu.CompilerParams(
            vmem_limit_bytes=VMEM, dimension_semantics=("arbitrary", "arbitrary")
        ),
        cost_estimate=pl.CostEstimate(
            flops=experts * 300 * depth * ff * 4,
            bytes_accessed=experts * depth * ff * 4,
            transcendentals=0,
        ),
        name="up_first" if first else "up_rest",
    )(meta, code, *xs, w_gate, w_up, *(() if first else partial))


def down_kernel(experts, block, meta, code, gate, h, wd, own, far, near, wt, tmp, stack):
    @pl.when(pl.program_id(0) == 0)
    def _():
        tmp[...] = jnp.zeros_like(tmp)
        rows = lax.broadcasted_iota(jnp.int32, (STEP, 256), 0)
        for k in range(4):
            for e in range(experts):
                hit = rows == code[e, k : k + 1, :]
                wt[k, e * STEP : (e + 1) * STEP, :] = jnp.where(
                    hit, gate[e, k : k + 1, :], 0.0
                ).astype(jnp.bfloat16)

    @pl.loop(0, experts)
    def _(e):
        total = meta[e * 8 + 4]
        size = (total + STEP - 1) // STEP
        for v in range(1, 5):

            @pl.when(size == v)
            def _(v=v):
                m = v * STEP
                out = jnp.dot(h[e, :m, :], wd[e], preferred_element_type=jnp.float32)
                tmp[:m, :] = out.astype(jnp.bfloat16)

        to = pl.ds(pl.multiple_of(e * STEP, STEP), STEP)
        for k in range(4):
            at = pl.multiple_of(meta[e * 8 + k], 16)
            stack[k, to, :] = tmp[pl.ds(at, STEP), :]

    def summed(k):
        return lax.dot_general(
            wt[k], stack[k], (((0,), (0,)), ((), ())), preferred_element_type=jnp.float32
        )

    own[...] = summed(0)
    far[...] = summed(2)
    near[0] = summed(1).astype(jnp.bfloat16)
    near[1] = summed(3).astype(jnp.bfloat16)


def down(meta, code, gate, h, w_down, start, columns, block):
    experts, ff, _ = w_down.shape
    once = pl.Buffered(1)
    return pl.pallas_call(
        functools.partial(down_kernel, experts, block),
        grid_spec=pltpu.PrefetchScalarGridSpec(
            num_scalar_prefetch=1,
            grid=(columns // block,),
            in_specs=[
                pl.BlockSpec((experts, 4, 256), lambda n, m: (0, 0, 0), pipeline_mode=once),
                pl.BlockSpec((experts, 4, 256), lambda n, m: (0, 0, 0), pipeline_mode=once),
                pl.BlockSpec((experts, 5 * STEP, ff), lambda n, m: (0, 0, 0), pipeline_mode=once),
                pl.BlockSpec((experts, ff, block), lambda n, m: (0, 0, n + start // block)),
            ],
            out_specs=[
                pl.BlockSpec((256, block), lambda n, m: (0, n)),
                pl.BlockSpec((256, block), lambda n, m: (0, n)),
                pl.BlockSpec((2, 256, block), lambda n, m: (0, 0, n)),
            ],
            scratch_shapes=[
                pltpu.VMEM((4, experts * STEP, 256), jnp.bfloat16),
                pltpu.VMEM((5 * STEP, block), jnp.bfloat16),
                pltpu.VMEM((4, experts * STEP, block), jnp.bfloat16),
            ],
        ),
        out_shape=[
            jax.ShapeDtypeStruct((256, columns), jnp.float32),
            jax.ShapeDtypeStruct((256, columns), jnp.float32),
            jax.ShapeDtypeStruct((2, 256, columns), jnp.bfloat16),
        ],
        compiler_params=pltpu.CompilerParams(
            vmem_limit_bytes=VMEM, dimension_semantics=("arbitrary",)
        ),
        cost_estimate=pl.CostEstimate(
            flops=experts * 300 * columns * ff * 2,
            bytes_accessed=experts * columns * ff * 2,
            transcendentals=0,
        ),
        name="down",
    )(meta, code, gate, h, w_down)


def layer(x, expert, slot, gate, w_gate, w_up, w_down, s_gate, s_up, s_down):
    local = w_gate.shape[0]
    experts = 4 * local
    x, expert, slot, gate = x[0, 0], expert[0, 0], slot[0, 0], gate[0, 0]
    tokens, top = expert.shape
    slots = 5 * tokens * top // (4 * experts)
    same = functools.partial(lax.ppermute, axis_name="ep", perm=SAME)
    cross = functools.partial(lax.ppermute, axis_name="ep", perm=CROSS)

    def everyone(v):
        far = cross(v)
        return [v, same(v), far, same(far)]

    table = tables(expert, slot, gate, experts, slots)
    table = jnp.stack(everyone(table))
    table = lax.dynamic_slice_in_dim(table, lax.axis_index("ep") * local, local, 2)
    code = table[:, 0].transpose(1, 0, 2).astype(jnp.int32)
    weight = table[:, 1].transpose(1, 0, 2)
    used = (jnp.max(code, -1) + 16) // 16 * 16
    ends = jnp.cumsum(used, 1)
    meta = jnp.concatenate([ends - used, ends[:, 3:], jnp.zeros((local, 3), jnp.int32)], 1)
    meta = meta.reshape(-1)

    x_first = everyone(x[:, :FIRST])
    x_rest = everyone(x[:, FIRST:])

    def dot(a, b):
        return jnp.dot(a, b, preferred_element_type=jnp.float32)

    hidden = (jax.nn.silu(dot(x, s_gate)) * dot(x, s_up)).astype(jnp.bfloat16)
    shared = dot(hidden, s_down)

    partial = up(meta, code, x_first, w_gate, w_up, 0, 1024)
    h = up(meta, code, x_rest, w_gate, w_up, FIRST, 512, partial)

    pieces, start = [], 0
    for columns in CHUNKS:
        own, far, near = down(meta, code, weight, h, w_down, start, columns, 512)
        near = same(near)
        far = cross((far + near[1].astype(jnp.float32)).astype(jnp.bfloat16))
        total = own + near[0].astype(jnp.float32) + far.astype(jnp.float32)
        total = total + shared[:, start : start + columns]
        pieces.append(total.astype(jnp.bfloat16))
        start += columns
    return jnp.concatenate(pieces, 1)[None, None]


def solution(mesh):
    rows, whole = P("dp", "ep"), P()
    return jax.shard_map(
        layer,
        mesh=mesh,
        in_specs=(rows,) * 4 + (P("ep"),) * 3 + (whole,) * 3,
        out_specs=rows,
        check_vma=False,
    )
```

time: 1240 us -> 568 us (0.46)
  blocking collectives: 437 us -> 0 us
  Pallas kernels: 0 us -> 335 us
  matrix products: 376 us -> 43.3 us
  waiting for transfers between devices: 384 us -> 124 us
  starting transfers between devices: 10.8 us -> 37.5 us
  local copies, waits for them, and re-layouts: 28.3 us -> 5.93 us
  other arithmetic: 0.01 us -> 17.3 us
    another operation x1 -> x0, blocking collectives: 437 us -> none  [placed(): return lax.with_sharding_constraint(v, NamedSharding(mesh, P(*spec)))]
    another operation x1 -> x0, waiting for transfers between devices: 384 us -> none  [placed(): return lax.with_sharding_constraint(v, NamedSharding(mesh, P(*spec)))]
    pallas_call x0 -> x5, Pallas kernels: none -> 335 us  [the longest x2 225 us: up(): pl.pallas_call(functools.partial(up_kernel, depth, block, first), grid_sp...]
    dot_general x10 -> x2, matrix products: 376 us -> 43.3 us  [dot(): return jnp.dot(a, b, preferred_element_type=jnp.float32)]
    ppermute x0 -> x15, waiting for transfers between devices: none -> 124 us  [the longest x3 76.7 us: everyone(): far = cross(v)]
    ppermute x0 -> x15, starting transfers between devices: none -> 37.5 us  [the longest x3 23.2 us: layer(): far = cross((far + near[1].astype(jnp.float32)).astype(jnp.bfloat16))]
    another operation x1 -> x5, local copies, waits for them, and re-layouts: 26.5 us -> 0.19 us  [the longest x4 0.19 us: layer(): table = jnp.stack(everyone(table))]
    convert_element_type x1 -> x6, other arithmetic: 0.01 us -> 14 us  [the longest x2 7.83 us: layer(): pieces.append(total.astype(jnp.bfloat16))]
  transfers between devices with their start and end apart: 1 -> 15, of which waited for: 1 -> 5; matrix products, arithmetic and copies ran while one was open for 3% -> 10% of each run, Pallas kernels for 0% -> 16%
where the time goes in v1:
time: 568 us; the launch traced here: 564 us
  Pallas kernels  335 us (59%)
  waiting for transfers between devices  124 us (22%)
  matrix products  43.3 us (8%)
  starting transfers between devices  37.5 us (7%)
  other arithmetic  17.3 us (3%)
  local copies, waits for them, and re-layouts  5.93 us (1%)
    pallas_call x2, Pallas kernels, up(): pl.pallas_call(functools.partial(up_kernel, depth, block, first), grid_sp...  225 us
    pallas_call x3, Pallas kernels, down(): pl.pallas_call(functools.partial(down_kernel, experts, block), grid_spec=...  110 us
    ppermute x3, waiting for transfers between devices, everyone(): far = cross(v)  76.7 us
    dot_general x2, matrix products, dot(): return jnp.dot(a, b, preferred_element_type=jnp.float32)  43.3 us
    ppermute x3, waiting for transfers between devices, layer(): far = cross((far + near[1].astype(jnp.float32)).astype(jnp.bfloat16))  42.5 us
    ppermute x3, starting transfers between devices, layer(): far = cross((far + near[1].astype(jnp.float32)).astype(jnp.bfloat16))  23.2 us
  transfers between devices with their start and end apart: 15, of which 5 were waited for; matrix products, arithmetic and copies ran while one was open for 10% of the time, Pallas kernels for 16%

profile of v1, /device:TPU:0, one launch (start us, length us, event | category | flops | bytes accessed | tf_op | source)
XLA Modules:
  0.0 563.6 jit_solution(4558132642166306398)
XLA Ops:
  0.0 3.4 slice.58.x0
  3.4 3.3 collective-permute-start.4
  6.8 1.3 slice.59.x0
  8.4 2.0 collective-permute-start.1
  10.4 76.7 %collective-permute-done.1 = f32[2,24,256]{2,1,0:T(8,128)S(1)} collective-permute-done((f32[2,24,256]{2,1,0:T(8,128)S(1)}, f32[2,24,256]{2,1,0:T(8,128)S(1)}, u32[]{:S(2)}, u32[]{:S(2)}) %collective-permute-start.1) | collective-permute-done | bytes 49184 | tf_op jit(solution)/shard_map/ppermute | solution.py:206
  90.8 4.4 collective-permute-done.8.x3
  95.2 71.0 %up_first.1 = (f32[6,448,2048]{2,1,0:T(8,128)}, f32[6,448,2048]{2,1,0:T(8,128)}) custom-call(s32[48]{0:T(128)} %reshape.38.meta, s32[6,4,256]{2,1,0:T(4,128)} %get-tuple-element.30.code, bf16[256,2048]{1,0:T(8,128)(2,1)} %copy-done, bf16[256,2048]{1,0:T(8,128)(2,1)} %collective-permute-done.6.x1, bf16[256,2048]{1,0:T(8,128)(2,1)} %copy-done.6, ...), custom_call_target="tpu_custom_call" | custom-call | flops 30198988800 | bytes 100663296 | tf_op jit(solution)/shard_map/up_first/pallas_call | solution.py:89
  166.2 154.2 %up_rest.1.h = bf16[6,560,2048]{2,1,0:T(8,128)(2,1)} custom-call(s32[48]{0:T(128)} %reshape.38.meta, s32[6,4,256]{2,1,0:T(4,128)} %get-tuple-element.30.code, bf16[256,5120]{1,0:T(8,128)(2,1)} %slice.58.x0, bf16[256,5120]{1,0:T(8,128)(2,1)} %collective-permute-done.3.x1, bf16[256,5120]{1,0:T(8,128)(2,1)} %collective-permute-done.4.x2, ...), custom_call_target="tpu_custom_call" | custom-call | flops 75497472000 | bytes 251658240 | tf_op jit(solution)/shard_map/up_rest/pallas_call | solution.py:89
  320.4 44.1 %down.5 = (f32[256,3072]{1,0:T(8,128)}, f32[256,3072]{1,0:T(8,128)}, bf16[2,256,3072]{2,1,0:T(8,128)(2,1)}) custom-call(s32[48]{0:T(128)} %reshape.38.meta, s32[6,4,256]{2,1,0:T(4,128)} %get-tuple-element.30.code, f32[6,4,256]{2,1,0:T(4,128)} %get-tuple-element.29.gate, bf16[6,560,2048]{2,1,0:T(8,128)(2,1)} %up_rest.1.h, bf16[6,2048,7168]{2,1,0:T(8,128)(2,1)} %wd.5), custom_call_target="tpu_custom_call" | custom-call | flops 22649241600 | bytes 75497472 | tf_op jit(solution)/shard_map/down/pallas_call | solution.py:157
  364.5 44.3 %down.4 = (f32[256,3072]{1,0:T(8,128)}, f32[256,3072]{1,0:T(8,128)}, bf16[2,256,3072]{2,1,0:T(8,128)(2,1)}) custom-call(s32[48]{0:T(128)} %reshape.38.meta, s32[6,4,256]{2,1,0:T(4,128)} %get-tuple-element.30.code, f32[6,4,256]{2,1,0:T(4,128)} %get-tuple-element.29.gate, bf16[6,560,2048]{2,1,0:T(8,128)(2,1)} %up_rest.1.h, bf16[6,2048,7168]{2,1,0:T(8,128)(2,1)} %wd.5), custom_call_target="tpu_custom_call" | custom-call | flops 22649241600 | bytes 75497472 | tf_op jit(solution)/shard_map/down/pallas_call | solution.py:157
  408.8 7.3 %collective-permute-start.13 = (bf16[2,256,3072]{2,1,0:T(8,128)(2,1)}, bf16[2,256,3072]{2,1,0:T(8,128)(2,1)}, u32[]{:S(2)}, u32[]{:S(2)}) collective-permute-start(bf16[2,256,3072]{2,1,0:T(8,128)(2,1)} %get-tuple-element.25), channel_id=1, source_target_pairs={{0,1},{1,0},{2,3},{3,2},{4,5},{5,4},{6,7},{7,6}} | collective-permute-start | bytes 9437192 | tf_op jit(solution)/shard_map/ppermute | solution.py:234
  416.1 21.7 %down.3 = (f32[256,1024]{1,0:T(8,128)}, f32[256,1024]{1,0:T(8,128)}, bf16[2,256,1024]{2,1,0:T(8,128)(2,1)}) custom-call(s32[48]{0:T(128)} %reshape.38.meta, s32[6,4,256]{2,1,0:T(4,128)} %get-tuple-element.30.code, f32[6,4,256]{2,1,0:T(4,128)} %get-tuple-element.29.gate, bf16[6,560,2048]{2,1,0:T(8,128)(2,1)} %up_rest.1.h, bf16[6,2048,7168]{2,1,0:T(8,128)(2,1)} %wd.5), custom_call_target="tpu_custom_call" | custom-call | flops 7549747200 | bytes 25165824 | tf_op jit(solution)/shard_map/down/pallas_call | solution.py:157
  438.4 15.5 %fusion.27 = f32[256,2048]{1,0:T(8,128)} fusion(bf16[7168,2048]{1,0:T(8,128)(2,1)} %param.17, bf16[1,1,256,7168]{3,2,1,0:T(8,128)(2,1)} %param.10), kind=kOutput, calls=%fused_computation.62 | convolution fusion | flops 7516192768 | bytes 35127296 | tf_op jit(solution)/shard_map/dot_general | solution.py:223
  453.9 1.1 fusion.14
  455.0 21.1 %collective-permute-start.10 = (bf16[256,1024]{1,0:T(8,128)(2,1)}, bf16[256,1024]{1,0:T(8,128)(2,1)}, u32[]{:S(2)}, u32[]{:S(2)}) collective-permute-start(bf16[256,1024]{1,0:T(8,128)(2,1)} %fusion.14), channel_id=1, source_target_pairs={{0,2},{1,3},{2,0},{3,1},{4,6},{5,7},{6,4},{7,5}} | collective-permute-start | bytes 1572872 | tf_op jit(solution)/shard_map/ppermute | solution.py:235
  476.1 3.2 fusion.2
  479.3 1.9 fusion.4
  481.4 2.0 collective-permute-start.12
  483.4 27.8 %fusion.7 = f32[256,7168]{1,0:T(8,128)} fusion(bf16[2048,7168]{1,0:T(8,128)(2,1)} %param.19, bf16[7168,2048]{1,0:T(8,128)(2,1)} %param.18, f32[256,2048]{1,0:T(8,128)} %fusion.27, bf16[1,1,256,7168]{3,2,1,0:T(8,128)(2,1)} %param.10), kind=kOutput, calls=%fused_computation.15 | convolution fusion | flops 15035531264 | bytes 71827456 | tf_op jit(solution)/shard_map/dot_general | solution.py:223
  511.2 2.3 fusion.13
  513.6 9.0 %collective-permute-done.14 = bf16[256,3072]{1,0:T(8,128)(2,1)} collective-permute-done((bf16[256,3072]{1,0:T(8,128)(2,1)}, bf16[256,3072]{1,0:T(8,128)(2,1)}, u32[]{:S(2)}, u32[]{:S(2)}) %collective-permute-start.14) | collective-permute-done | bytes 1572896 | tf_op jit(solution)/shard_map/ppermute | solution.py:235
  522.6 33.5 %collective-permute-done.12 = bf16[256,3072]{1,0:T(8,128)(2,1)} collective-permute-done((bf16[256,3072]{1,0:T(8,128)(2,1)}, bf16[256,3072]{1,0:T(8,128)(2,1)}, u32[]{:S(2)}, u32[]{:S(2)}) %collective-permute-start.12) | collective-permute-done | bytes 1572896 | tf_op jit(solution)/shard_map/ppermute | solution.py:235
  556.1 5.5 fusion.1
  561.6 2.0 maximum_bitcast_fusion
  (66 shorter events, 4.5 us)
Async XLA Ops:
  0.0 8.2 %copy-start.9 = (s32[1,1,256,8]{2,3,1,0:T(8,128)S(1)}, s32[1,1,256,8]{2,3,1,0:T(8,128)}, u32[]{:S(2)}) copy-start(s32[1,1,256,8]{2,3,1,0:T(8,128)} %param.12) | copy-start | bytes 24580
  0.0 8.2 %copy-start.10 = (s32[1,1,256,8]{2,3,1,0:T(8,128)S(1)}, s32[1,1,256,8]{2,3,1,0:T(8,128)}, u32[]{:S(2)}) copy-start(s32[1,1,256,8]{2,3,1,0:T(8,128)} %param.11) | copy-start | bytes 24580
  0.0 8.3 %copy-start.11 = (f32[1,1,256,8]{2,3,1,0:T(8,128)S(1)}, f32[1,1,256,8]{2,3,1,0:T(8,128)}, u32[]{:S(2)}) copy-start(f32[1,1,256,8]{2,3,1,0:T(8,128)} %param.13) | copy-start | bytes 24580
  3.4 87.0 %collective-permute-start.4 = (bf16[256,5120]{1,0:T(8,128)(2,1)}, bf16[256,5120]{1,0:T(8,128)(2,1)}, u32[]{:S(2)}, u32[]{:S(2)}) collective-permute-start(bf16[256,5120]{1,0:T(8,128)(2,1)} %slice.58.x0), channel_id=1, source_target_pairs={{0,2},{1,3},{2,0},{3,1},{4,6},{5,7},{6,4},{7,5}} | collective-permute-start | bytes 7864328 | tf_op jit(solution)/shard_map/ppermute | solution.py:206
  8.1 87.1 %copy-start = (bf16[256,2048]{1,0:T(8,128)(2,1)}, bf16[256,2048]{1,0:T(8,128)(2,1)S(1)}, u32[]{:S(2)}) copy-start(bf16[256,2048]{1,0:T(8,128)(2,1)S(1)} %slice.59.x0) | copy-start | bytes 3145732
  8.1 80.3 %collective-permute-start.7 = (bf16[256,2048]{1,0:T(8,128)(2,1)S(1)}, bf16[256,2048]{1,0:T(8,128)(2,1)S(1)}, u32[]{:S(2)}, u32[]{:S(2)}) collective-permute-start(bf16[256,2048]{1,0:T(8,128)(2,1)S(1)} %slice.59.x0), channel_id=1, source_target_pairs={{0,2},{1,3},{2,0},{3,1},{4,6},{5,7},{6,4},{7,5}} | collective-permute-start | bytes 3145736 | tf_op jit(solution)/shard_map/ppermute | solution.py:206
  8.4 78.7 %collective-permute-start.1 = (f32[2,24,256]{2,1,0:T(8,128)S(1)}, f32[2,24,256]{2,1,0:T(8,128)S(1)}, u32[]{:S(2)}, u32[]{:S(2)}) collective-permute-start(f32[2,24,256]{2,1,0:T(8,128)S(1)} %get-tuple-element.31), channel_id=1, source_target_pairs={{0,2},{1,3},{2,0},{3,1},{4,6},{5,7},{6,4},{7,5}} | collective-permute-start | bytes 147464 | tf_op jit(solution)/shard_map/ppermute | solution.py:206
  10.4 77.4 %collective-permute-start = (f32[2,24,256]{2,1,0:T(8,128)S(1)}, f32[2,24,256]{2,1,0:T(8,128)S(1)}, u32[]{:S(2)}, u32[]{:S(2)}) collective-permute-start(f32[2,24,256]{2,1,0:T(8,128)S(1)} %get-tuple-element.31), channel_id=1, source_target_pairs={{0,1},{1,0},{2,3},{3,2},{4,5},{5,4},{6,7},{7,6}} | collective-permute-start | bytes 147464 | tf_op jit(solution)/shard_map/ppermute | solution.py:207
  87.2 1.2 collective-permute-start.2
  87.2 3.6 collective-permute-start.6
  87.9 78.3 %collective-permute-start.3 = (bf16[256,5120]{1,0:T(8,128)(2,1)}, bf16[256,5120]{1,0:T(8,128)(2,1)}, u32[]{:S(2)}, u32[]{:S(2)}) collective-permute-start(bf16[256,5120]{1,0:T(8,128)(2,1)} %slice.58.x0), channel_id=1, source_target_pairs={{0,1},{1,0},{2,3},{3,2},{4,5},{5,4},{6,7},{7,6}} | collective-permute-start | bytes 7864328 | tf_op jit(solution)/shard_map/ppermute | solution.py:207
  88.5 6.8 %collective-permute-start.8 = (bf16[256,2048]{1,0:T(8,128)(2,1)S(1)}, bf16[256,2048]{1,0:T(8,128)(2,1)}, u32[]{:S(2)}, u32[]{:S(2)}) collective-permute-start(bf16[256,2048]{1,0:T(8,128)(2,1)S(1)} %collective-permute-done.7.x2), channel_id=1, source_target_pairs={{0,1},{1,0},{2,3},{3,2},{4,5},{5,4},{6,7},{7,6}} | collective-permute-start | bytes 3145736 | tf_op jit(solution)/shard_map/ppermute | solution.py:207
  90.5 75.8 %collective-permute-start.5 = (bf16[256,5120]{1,0:T(8,128)(2,1)}, bf16[256,5120]{1,0:T(8,128)(2,1)}, u32[]{:S(2)}, u32[]{:S(2)}) collective-permute-start(bf16[256,5120]{1,0:T(8,128)(2,1)} %collective-permute-done.4.x2), channel_id=1, source_target_pairs={{0,1},{1,0},{2,3},{3,2},{4,5},{5,4},{6,7},{7,6}} | collective-permute-start | bytes 7864328 | tf_op jit(solution)/shard_map/ppermute | solution.py:207
  408.8 67.3 %collective-permute-start.13 = (bf16[2,256,3072]{2,1,0:T(8,128)(2,1)}, bf16[2,256,3072]{2,1,0:T(8,128)(2,1)}, u32[]{:S(2)}, u32[]{:S(2)}) collective-permute-start(bf16[2,256,3072]{2,1,0:T(8,128)(2,1)} %get-tuple-element.25), channel_id=1, source_target_pairs={{0,1},{1,0},{2,3},{3,2},{4,5},{5,4},{6,7},{7,6}} | collective-permute-start | bytes 9437192 | tf_op jit(solution)/shard_map/ppermute | solution.py:234
  437.9 16.0 %collective-permute-start.9 = (bf16[2,256,1024]{2,1,0:T(8,128)(2,1)}, bf16[2,256,1024]{2,1,0:T(8,128)(2,1)S(1)}, u32[]{:S(2)}, u32[]{:S(2)}) collective-permute-start(bf16[2,256,1024]{2,1,0:T(8,128)(2,1)} %get-tuple-element.19), channel_id=1, source_target_pairs={{0,1},{1,0},{2,3},{3,2},{4,5},{5,4},{6,7},{7,6}} | collective-permute-start | bytes 3145736 | tf_op jit(solution)/shard_map/ppermute | solution.py:234
  438.3 15.5 %copy-start.8 = (f32[256,1024]{1,0:T(8,128)S(1)}, f32[256,1024]{1,0:T(8,128)}, u32[]{:S(2)}) copy-start(f32[256,1024]{1,0:T(8,128)} %get-tuple-element.20) | copy-start | bytes 3145732
  438.3 41.0 %collective-permute-start.11 = (bf16[2,256,3072]{2,1,0:T(8,128)(2,1)}, bf16[2,256,3072]{2,1,0:T(8,128)(2,1)S(1)}, u32[]{:S(2)}, u32[]{:S(2)}) collective-permute-start(bf16[2,256,3072]{2,1,0:T(8,128)(2,1)} %get-tuple-element.22), channel_id=1, source_target_pairs={{0,1},{1,0},{2,3},{3,2},{4,5},{5,4},{6,7},{7,6}} | collective-permute-start | bytes 9437192 | tf_op jit(solution)/shard_map/ppermute | solution.py:234
  438.4 37.7 %copy-start.2 = (f32[256,3072]{1,0:T(8,128)S(1)}, f32[256,3072]{1,0:T(8,128)}, u32[]{:S(2)}) copy-start(f32[256,3072]{1,0:T(8,128)} %get-tuple-element.26) | copy-start | bytes 9437188
  453.9 25.4 %copy-start.7 = (bf16[2,256,1024]{2,1,0:T(8,128)(2,1)}, bf16[2,256,1024]{2,1,0:T(8,128)(2,1)S(1)}, u32[]{:S(2)}) copy-start(bf16[2,256,1024]{2,1,0:T(8,128)(2,1)S(1)} %collective-permute-done.9) | copy-start | bytes 3145732
  455.0 56.3 %collective-permute-start.10 = (bf16[256,1024]{1,0:T(8,128)(2,1)}, bf16[256,1024]{1,0:T(8,128)(2,1)}, u32[]{:S(2)}, u32[]{:S(2)}) collective-permute-start(bf16[256,1024]{1,0:T(8,128)(2,1)} %fusion.14), channel_id=1, source_target_pairs={{0,2},{1,3},{2,0},{3,1},{4,6},{5,7},{6,4},{7,5}} | collective-permute-start | bytes 1572872 | tf_op jit(solution)/shard_map/ppermute | solution.py:235
  479.3 43.3 %collective-permute-start.14 = (bf16[256,3072]{1,0:T(8,128)(2,1)}, bf16[256,3072]{1,0:T(8,128)(2,1)}, u32[]{:S(2)}, u32[]{:S(2)}) collective-permute-start(bf16[256,3072]{1,0:T(8,128)(2,1)} %fusion.2), channel_id=1, source_target_pairs={{0,2},{1,3},{2,0},{3,1},{4,6},{5,7},{6,4},{7,5}} | collective-permute-start | bytes 4718600 | tf_op jit(solution)/shard_map/ppermute | solution.py:235
  481.4 74.7 %collective-permute-start.12 = (bf16[256,3072]{1,0:T(8,128)(2,1)}, bf16[256,3072]{1,0:T(8,128)(2,1)}, u32[]{:S(2)}, u32[]{:S(2)}) collective-permute-start(bf16[256,3072]{1,0:T(8,128)(2,1)} %fusion.4), channel_id=1, source_target_pairs={{0,2},{1,3},{2,0},{3,1},{4,6},{5,7},{6,4},{7,5}} | collective-permute-start | bytes 4718600 | tf_op jit(solution)/shard_map/ppermute | solution.py:235
  483.4 72.7 %copy-start.4 = (f32[256,3072]{1,0:T(8,128)S(1)}, f32[256,3072]{1,0:T(8,128)}, u32[]{:S(2)}) copy-start(f32[256,3072]{1,0:T(8,128)} %get-tuple-element.21) | copy-start | bytes 9437188
  511.2 44.9 %copy-start.3 = (f32[256,3072]{1,0:T(8,128)S(1)}, f32[256,3072]{1,0:T(8,128)}, u32[]{:S(2)}) copy-start(f32[256,3072]{1,0:T(8,128)} %get-tuple-element.24) | copy-start | bytes 9437188
  (3 other events, 7.7 us)

commit v2 on v1

v2 whole, which is shorter than its diff:
```python
import functools

import jax
import jax.numpy as jnp
from jax import lax
from jax.experimental import pallas as pl
from jax.experimental.pallas import tpu as pltpu
from jax.sharding import PartitionSpec as P

SAME = [(0, 1), (1, 0), (2, 3), (3, 2)]
CROSS = [(0, 2), (1, 3), (2, 0), (3, 1)]
STEP = 112
EARLY = 2
CHUNKS = (1024, 3072, 3072)
VMEM = 63 * 2**20
KB = 1024
F32, BF16 = jnp.float32, jnp.bfloat16


def silu(g):
    return g / (1.0 + jnp.exp(-g))


def dot(a, b):
    return jnp.dot(a, b, preferred_element_type=F32)


def tables(expert, slot, gate, experts, slots):
    expert, slot, gate = expert.T, slot.T, gate.T
    hit = (expert[None] == jnp.arange(experts)[:, None, None]) & (slot < slots)[None]
    code = jnp.sum(jnp.where(hit, slot[None] + 1, 0), 1) - 1
    weight = jnp.sum(jnp.where(hit, gate[None], 0.0), 1)
    return jnp.stack([code.astype(F32), weight])


def arrive_kernel(
    local, x, table, w_gate, w_up, s_gate, s_up, s_down,
    xs, tabs, h, shared,
    got, tab, ring, ring2, acc_s, acc, z, hidden, stage,
    ring_sem, ring2_sem, stage_sem, cross_send, cross_recv, pass_send, pass_recv,
    own_send, own_recv, tab_send, tab_recv, out_sem,
):
    d, ff = x.shape[1], s_gate.shape[1]
    chunks = d // KB
    me = lax.axis_index("ep")
    partner, across = me + 1 - 2 * lax.rem(me, 2), lax.rem(me + 2, 4)
    peers = (partner, across, 3 - me)

    barrier = pltpu.get_barrier_semaphore()
    for peer in peers:
        pl.semaphore_signal(
            barrier, inc=1, device_id={"ep": peer}, device_id_type=pl.DeviceIdType.MESH
        )
    pl.semaphore_wait(barrier, 3)

    def remote(src, dst, send, recv, peer):
        return pltpu.make_async_remote_copy(
            src, dst, send, recv, device_id={"ep": peer}, device_id_type=pl.DeviceIdType.MESH
        )

    def columns(k):
        return pl.ds(pl.multiple_of(k * KB, KB), KB)

    def cross(k):
        c = columns(k)
        return remote(x.at[:, c], got.at[1, :, c], cross_send.at[k], cross_recv.at[k], across)

    def onward(k):
        c = columns(k)
        return remote(
            got.at[1, :, c], got.at[2, :, c], pass_send.at[k], pass_recv.at[k], partner
        )

    own = remote(x, got.at[0], own_send, own_recv, partner)
    tab_copies = [
        remote(table, tab.at[i], tab_send.at[i], tab_recv.at[i], peer)
        for i, peer in enumerate(peers)
    ]

    def keep(i, k):
        c = columns(k)
        return pltpu.make_async_copy(got.at[i, :, c], xs.at[i, :, c], out_sem.at[i, k])

    n_shared = 2 * chunks
    n_all = n_shared + 2 * EARLY * chunks
    slots = ring.shape[0]

    def fetch(j):
        slot = lax.rem(j, slots)

        def go(src):
            pltpu.make_async_copy(src, ring.at[slot], ring_sem.at[slot]).start()

        for i, w in enumerate((s_gate, s_up)):

            @pl.when((j < n_shared) & (lax.rem(j, 2) == i))
            def _(w=w):
                go(w.at[columns(j // 2), :])

        i = jnp.maximum(j - n_shared, 0)
        k, q = i // (2 * EARLY), lax.rem(i, 2 * EARLY)
        for s, w in enumerate((w_gate, w_up)):

            @pl.when((j >= n_shared) & (j < n_all) & (lax.rem(q, 2) == s))
            def _(w=w):
                go(w.at[q // 2, columns(k), :])

    def ready(j):
        slot = lax.rem(j, slots)
        pltpu.make_async_copy(s_gate.at[:KB, :], ring.at[slot], ring_sem.at[slot]).wait()
        return slot

    wide = ring2.shape[2]

    def down_tile(n):
        slot = lax.rem(n, 2)
        c = pl.ds(pl.multiple_of(n * wide, wide), wide)
        return pltpu.make_async_copy(s_down.at[:, c], ring2.at[slot], ring2_sem.at[slot])

    def put(n):
        slot = lax.rem(n, 2)
        c = pl.ds(pl.multiple_of(n * wide, wide), wide)
        return pltpu.make_async_copy(stage.at[slot], shared.at[:, c], stage_sem.at[slot])

    for copy in tab_copies:
        copy.start()

    @pl.loop(0, chunks)
    def _(k):
        cross(k).start()

    own.start()
    for j in range(slots):
        fetch(jnp.int32(j))
    down_tile(0).start()
    down_tile(1).start()

    acc_s[...] = jnp.zeros_like(acc_s)

    @pl.loop(0, n_shared)
    def _(j):
        slot = ready(j)
        a = x[:, columns(j // 2)]
        side = lax.rem(j, 2)
        for n in range(ff // 512):
            c = slice(n * 512, n * 512 + 512)
            acc_s[side, :, c] += dot(a, ring[slot, :, c])
        fetch(j + slots)

    for n in range(ff // 512):
        c = slice(n * 512, n * 512 + 512)
        hidden[:, c] = (silu(acc_s[0, :, c]) * acc_s[1, :, c]).astype(BF16)

    n_down = d // wide

    @pl.loop(0, n_down)
    def _(n):
        down_tile(n).wait()

        @pl.when(n >= 2)
        def _():
            put(n - 2).wait()

        slot = lax.rem(n, 2)
        stage[slot] = dot(hidden[...], ring2[slot])

        @pl.when(n + 2 < n_down)
        def _():
            down_tile(n + 2).start()

        put(n).start()

    put(n_down - 2).wait()
    put(n_down - 1).wait()

    for copy in tab_copies:
        copy.wait()
    tabs[0] = table[...]
    for i in range(3):
        tabs[1 + i] = tab[i]
    own.wait()

    acc[...] = jnp.zeros_like(acc)
    rows = lax.broadcasted_iota(jnp.int32, (STEP, 256), 0).astype(F32)

    @pl.loop(0, chunks)
    def _(k):
        c = columns(k)
        cross(k).wait_recv()
        onward(k).start()
        keep(0, k).start()
        keep(1, k).start()

        def picked(i, a):
            parts = []
            for e in range(EARLY):
                t = table if i == 0 else tab.at[i - 1]
                code = t[0, pl.ds(me * local + e, 1), :]
                parts.append((rows == code).astype(BF16))
            z_i = dot(jnp.concatenate(parts, 0), a).astype(BF16)
            for e in range(EARLY):
                z[e, i * STEP : (i + 1) * STEP, :] = z_i[e * STEP : (e + 1) * STEP, :]

        picked(0, x[:, c])
        picked(1, got[0, :, c])
        picked(2, got[1, :, c])
        onward(k).wait_recv()
        keep(2, k).start()
        picked(3, got[2, :, c])

        @pl.loop(0, 2 * EARLY)
        def _(q):
            j = n_shared + 2 * EARLY * k + q
            slot = ready(j)
            for n in range(ff // 512):
                cc = slice(n * 512, n * 512 + 512)
                acc[q, :, cc] += dot(z[q // 2], ring[slot, :, cc])
            fetch(j + slots)

    for e in range(EARLY):
        for n in range(ff // 512):
            c = slice(n * 512, n * 512 + 512)
            g, u = acc[2 * e, :, c], acc[2 * e + 1, :, c]
            h[e, :, c] = (silu(g) * u).astype(BF16)

    @pl.loop(0, chunks)
    def _(k):
        cross(k).wait_send()
        onward(k).wait_send()
        for i in range(3):
            keep(i, k).wait()


def arrive(x, table, w_gate, w_up, s_gate, s_up, s_down):
    tokens, d = x.shape
    local, _, ff = w_gate.shape
    chunks = d // KB
    vmem, hbm = pl.BlockSpec(memory_space=pltpu.VMEM), pl.BlockSpec(memory_space=pl.ANY)
    dma = pltpu.SemaphoreType.DMA
    return pl.pallas_call(
        functools.partial(arrive_kernel, local),
        in_specs=[vmem] * 2 + [hbm] * 5,
        out_specs=[hbm, vmem, vmem, hbm],
        out_shape=[
            jax.ShapeDtypeStruct((3, tokens, d), BF16),
            jax.ShapeDtypeStruct((4, *table.shape), F32),
            jax.ShapeDtypeStruct((EARLY, 4 * STEP, ff), BF16),
            jax.ShapeDtypeStruct((tokens, d), F32),
        ],
        scratch_shapes=[
            pltpu.VMEM((3, tokens, d), BF16),
            pltpu.VMEM((3, *table.shape), F32),
            pltpu.VMEM((3, KB, ff), BF16),
            pltpu.VMEM((2, ff, 512), BF16),
            pltpu.VMEM((2, tokens, ff), F32),
            pltpu.VMEM((2 * EARLY, 4 * STEP, ff), F32),
            pltpu.VMEM((EARLY, 4 * STEP, KB), BF16),
            pltpu.VMEM((tokens, ff), BF16),
            pltpu.VMEM((2, tokens, 512), F32),
            dma((3,)), dma((2,)), dma((2,)),
            dma((chunks,)), dma((chunks,)), dma((chunks,)), dma((chunks,)),
            dma, dma, dma((3,)), dma((3,)), dma((3, chunks)),
        ],
        compiler_params=pltpu.CompilerParams(
            collective_id=0, has_side_effects=True, vmem_limit_bytes=VMEM
        ),
        name="arrive",
    )(x, table, w_gate, w_up, s_gate, s_up, s_down)


def up_kernel(block, meta, code, x0, x1, wg, wu, h_out, z):
    depth = x0.shape[1]
    e, n = pl.program_id(0), pl.program_id(1)
    at_meta = (e + EARLY) * 8
    total = pl.multiple_of(meta[at_meta + 4], 16)

    @pl.when(n == 0)
    def _():
        rows = lax.broadcasted_iota(jnp.int32, (STEP, 256), 0)
        picks = [(rows == code[0, k : k + 1, :]).astype(BF16) for k in range(4)]

        @pl.loop(0, depth // 1024)
        def _(c):
            cols = pl.ds(pl.multiple_of(c * 1024, 1024), 1024)
            parts = [
                dot(picks[k], x0[:, cols] if k == 0 else x1[k - 1, :, cols]).astype(BF16)
                for k in range(4)
            ]
            for k in range(4):
                at = pl.multiple_of(meta[at_meta + k], 16)
                z[pl.ds(at, STEP), cols] = parts[k]

        z[pl.ds(total, STEP), :] = jnp.zeros((STEP, depth), BF16)

    size = (total + STEP - 1) // STEP
    for v in range(1, 5):

        @pl.when(size == v)
        def _(v=v):
            m = v * STEP
            g = dot(z[:m, :], wg[0])
            u = dot(z[:m, :], wu[0])
            h_out[0, :m, :] = (silu(g) * u).astype(BF16)


def up(meta, code, x0, x1, w_gate, w_up, block):
    experts, depth, ff = w_gate.shape
    late = experts - EARLY
    once = pl.Buffered(1)
    weight = pl.BlockSpec((1, depth, block), lambda e, n, m: (e + EARLY, 0, n))
    return pl.pallas_call(
        functools.partial(up_kernel, block),
        grid_spec=pltpu.PrefetchScalarGridSpec(
            num_scalar_prefetch=1,
            grid=(late, ff // block),
            in_specs=[
                pl.BlockSpec((1, 4, 256), lambda e, n, m: (e + EARLY, 0, 0)),
                pl.BlockSpec((256, depth), lambda e, n, m: (0, 0), pipeline_mode=once),
                pl.BlockSpec((3, 256, depth), lambda e, n, m: (0, 0, 0), pipeline_mode=once),
                weight,
                weight,
            ],
            out_specs=pl.BlockSpec((1, 4 * STEP, block), lambda e, n, m: (e, 0, n)),
            scratch_shapes=[pltpu.VMEM((5 * STEP, depth), BF16)],
        ),
        out_shape=jax.ShapeDtypeStruct((late, 4 * STEP, ff), BF16),
        compiler_params=pltpu.CompilerParams(
            vmem_limit_bytes=VMEM, dimension_semantics=("arbitrary", "arbitrary")
        ),
        cost_estimate=pl.CostEstimate(
            flops=late * 300 * depth * ff * 4,
            bytes_accessed=late * depth * ff * 4,
            transcendentals=0,
        ),
        name="up",
    )(meta, code, x0, x1, w_gate, w_up)


def down_kernel(experts, meta, code, gate, early, late, wd, own, far, near, h, wt, tmp, stack, sem):
    first = pl.program_id(0) == 0

    def load(e):
        if e < EARLY:
            return pltpu.make_async_copy(early.at[e], h.at[e], sem.at[e])
        return pltpu.make_async_copy(late.at[e - EARLY], h.at[e], sem.at[e])

    @pl.when(first)
    def _():
        for e in range(experts):
            load(e).start()
        tmp[...] = jnp.zeros_like(tmp)
        stack[...] = jnp.zeros_like(stack)
        rows = lax.broadcasted_iota(jnp.int32, (STEP, 256), 0)
        for k in range(4):
            parts = [
                jnp.where(rows == code[e, k : k + 1, :], gate[e, k : k + 1, :], 0.0)
                for e in range(experts)
            ]
            parts.append(jnp.zeros((stack.shape[1] - experts * STEP, 256), F32))
            wt[k] = jnp.concatenate(parts, 0).T.astype(BF16)
        for e in range(experts):
            load(e).wait()

    @pl.loop(0, experts)
    def _(e):
        total = meta[e * 8 + 4]
        size = (total + STEP - 1) // STEP
        for v in range(1, 5):

            @pl.when(size == v)
            def _(v=v):
                m = v * STEP
                tmp[:m, :] = dot(h[e, :m, :], wd[e]).astype(BF16)

        to = pl.ds(pl.multiple_of(e * STEP, STEP), STEP)
        for k in range(4):
            at = pl.multiple_of(meta[e * 8 + k], 16)
            stack[k, to, :] = tmp[pl.ds(at, STEP), :]

    near[0] = dot(wt[1], stack[1]).astype(BF16)
    near[1] = dot(wt[3], stack[3]).astype(BF16)
    far[...] = dot(wt[2], stack[2])
    own[...] = dot(wt[0], stack[0])


def down(meta, code, gate, early, late, w_down, start, columns, block):
    experts, ff, _ = w_down.shape
    once = pl.Buffered(1)
    small = pl.BlockSpec((experts, 4, 256), lambda n, m: (0, 0, 0), pipeline_mode=once)
    depth = -(-experts * STEP // 256) * 256
    return pl.pallas_call(
        functools.partial(down_kernel, experts),
        grid_spec=pltpu.PrefetchScalarGridSpec(
            num_scalar_prefetch=1,
            grid=(columns // block,),
            in_specs=[
                small,
                small,
                pl.BlockSpec(memory_space=pl.ANY),
                pl.BlockSpec(memory_space=pl.ANY),
                pl.BlockSpec((experts, ff, block), lambda n, m: (0, 0, n + start // block)),
            ],
            out_specs=[
                pl.BlockSpec((256, block), lambda n, m: (0, n)),
                pl.BlockSpec((256, block), lambda n, m: (0, n)),
                pl.BlockSpec((2, 256, block), lambda n, m: (0, 0, n)),
            ],
            scratch_shapes=[
                pltpu.VMEM((experts, 4 * STEP, ff), BF16),
                pltpu.VMEM((4, 256, depth), BF16),
                pltpu.VMEM((5 * STEP, block), BF16),
                pltpu.VMEM((4, depth, block), BF16),
                pltpu.SemaphoreType.DMA((experts,)),
            ],
        ),
        out_shape=[
            jax.ShapeDtypeStruct((256, columns), F32),
            jax.ShapeDtypeStruct((256, columns), F32),
            jax.ShapeDtypeStruct((2, 256, columns), BF16),
        ],
        compiler_params=pltpu.CompilerParams(
            vmem_limit_bytes=VMEM, dimension_semantics=("arbitrary",)
        ),
        cost_estimate=pl.CostEstimate(
            flops=experts * 300 * columns * ff * 2,
            bytes_accessed=experts * columns * ff * 2,
            transcendentals=0,
        ),
        name="down",
    )(meta, code, gate, early, late, w_down)


def layer(x, expert, slot, gate, w_gate, w_up, w_down, s_gate, s_up, s_down):
    local = w_gate.shape[0]
    experts = 4 * local
    x, expert, slot, gate = x[0, 0], expert[0, 0], slot[0, 0], gate[0, 0]
    tokens, top = expert.shape
    slots = 5 * tokens * top // (4 * experts)
    same = functools.partial(lax.ppermute, axis_name="ep", perm=SAME)
    cross = functools.partial(lax.ppermute, axis_name="ep", perm=CROSS)

    table = tables(expert, slot, gate, experts, slots)
    xs, table, early, shared = arrive(x, table, w_gate, w_up, s_gate, s_up, s_down)
    table = lax.dynamic_slice_in_dim(table, lax.axis_index("ep") * local, local, 2)
    code = table[:, 0].transpose(1, 0, 2).astype(jnp.int32)
    weight = table[:, 1].transpose(1, 0, 2)
    used = (jnp.max(code, -1) + 16) // 16 * 16
    used = jnp.where(jnp.arange(local)[:, None] < EARLY, STEP, used)
    starts = [jnp.zeros_like(used[:, 0])]
    for k in range(4):
        starts.append(starts[-1] + used[:, k])
    meta = jnp.stack(starts + starts[:3], 1).reshape(-1)

    late = up(meta, code, x, xs, w_gate, w_up, 512)

    pieces, start = [], 0
    for columns in CHUNKS:
        own, far, near = down(meta, code, weight, early, late, w_down, start, columns, 512)
        meta, own = lax.optimization_barrier((meta, own))
        near = same(near)
        far = cross((far + near[1].astype(F32)).astype(BF16))
        total = own + near[0].astype(F32) + far.astype(F32)
        total = total + shared[:, start : start + columns]
        pieces.append(total.astype(BF16))
        start += columns
    return jnp.concatenate(pieces, 1)[None, None]


def solution(mesh):
    rows, whole = P("dp", "ep"), P()
    return jax.shard_map(
        layer,
        mesh=mesh,
        in_specs=(rows,) * 4 + (P("ep"),) * 3 + (whole,) * 3,
        out_specs=rows,
        check_vma=False,
    )
```

time: 568 us -> 493 us (0.87)
  Pallas kernels: 335 us -> 385 us
  matrix products: 43.3 us -> 0 us
  waiting for transfers between devices: 124 us -> 81.7 us
  starting transfers between devices: 37.5 us -> 2.65 us
    pallas_call x5, Pallas kernels: 335 us -> 385 us  [the longest x3 143 us: down(): pl.pallas_call(functools.partial(down_kernel, experts), grid_spec=pltpu.P...]
    ppermute x12 -> x3, waiting for transfers between devices: 124 us -> 74.7 us  [layer(): far = cross((far + near[1].astype(F32)).astype(BF16))]
    dot_general x2 -> x0, matrix products: 43.3 us -> none  [dot(): return jnp.dot(a, b, preferred_element_type=jnp.float32)]
    ppermute x12 -> x3, starting transfers between devices: 29.6 us -> 2.09 us  [layer(): far = cross((far + near[1].astype(F32)).astype(BF16))]
    ppermute x3, starting transfers between devices: 7.85 us -> 0.56 us  [layer(): near = same(near)]
    ppermute x3, waiting for transfers between devices: 0.01 us -> 7.05 us  [layer(): near = same(near)]
    convert_element_type x6, other arithmetic: 14 us -> 7.45 us  [the longest x3 5.19 us: layer(): far = cross((far + near[1].astype(F32)).astype(BF16))]
  transfers between devices with their start and end apart: 15 -> 6, of which waited for: 5 -> 3; matrix products, arithmetic and copies ran while one was open for 10% -> 1% of each run, Pallas kernels for 16% -> 0%
where the time goes in v2:
time: 493 us; the launch traced here: 486 us
  Pallas kernels  385 us (78%)
  waiting for transfers between devices  81.7 us (17%)
  other arithmetic  13.9 us (3%)
    pallas_call x3, Pallas kernels, down(): pl.pallas_call(functools.partial(down_kernel, experts), grid_spec=pltpu.P...  143 us
    pallas_call x1, Pallas kernels, up(): pl.pallas_call(functools.partial(up_kernel, block), grid_spec=pltpu.Prefe...  121 us
    pallas_call x1, Pallas kernels, arrive(): pl.pallas_call(functools.partial(arrive_kernel, local), in_specs=[vmem] *...  121 us
    ppermute x3, waiting for transfers between devices, layer(): far = cross((far + near[1].astype(F32)).astype(BF16))  74.7 us
  transfers between devices with their start and end apart: 6, of which 3 were waited for; matrix products, arithmetic and copies ran while one was open for 1% of the time, Pallas kernels for 0%

profile of v2, /device:TPU:0, one launch (start us, length us, event | category | flops | bytes accessed | tf_op | source)
XLA Modules:
  0.0 486.1 jit_solution(8506572866848353644)
XLA Ops:
  0.0 0.7 compare_bitcast_fusion
  0.7 0.7 add_bitcast_fusion
  1.4 0.8 select_reduce_fusion.1
  2.2 0.8 select_reduce_fusion
  3.0 0.6 pad_maximum_fusion.table
  3.6 121.0 %arrive.1 = (bf16[3,256,7168]{2,1,0:T(8,128)(2,1)}, f32[4,2,24,256]{3,2,1,0:T(8,128)}, bf16[2,448,2048]{2,1,0:T(8,128)(2,1)}, f32[256,7168]{1,0:T(8,128)}) custom-call(bf16[256,7168]{1,0:T(8,128)(2,1)} %bitcast.59, f32[2,24,256]{2,1,0:T(8,128)} %pad_maximum_fusion.table, bf16[6,7168,2048]{2,1,0:T(8,128)(2,1)} %wg.1, bf16[6,7168,2048]{2,1,0:T(8,128)(2,1)} %wu.1, ...), custom_call_target="tpu_custom_call" | custom-call | tf_op jit(solution)/shard_map/arrive/pallas_call | solution.py:240
  124.6 1.1 copy.12
  125.6 0.6 fusion.18
  126.3 0.6 dynamic-slice_bitcast_fusion.gate
  127.2 0.6 reshape.43.meta
  127.8 121.4 %up.1.late = bf16[4,448,2048]{2,1,0:T(8,128)(2,1)} custom-call(s32[48]{0:T(128)} %reshape.43.meta, s32[6,4,256]{2,1,0:T(4,128)} %get-tuple-element.44.code, bf16[256,7168]{1,0:T(8,128)(2,1)} %bitcast.60, bf16[3,256,7168]{2,1,0:T(8,128)(2,1)} %get-tuple-element.25.x1, bf16[6,7168,2048]{2,1,0:T(8,128)(2,1)} %wg.1, bf16[6,7168,2048]{2,1,0:T(8,128)(2,1)} %wu.1), custom_call_target="tpu_custom_call" | custom-call | flops 70464307200 | bytes 234881024 | tf_op jit(solution)/shard_map/up/pallas_call | solution.py:311
  249.2 28.2 %down.3 = (f32[256,1024]{1,0:T(8,128)}, f32[256,1024]{1,0:T(8,128)}, bf16[2,256,1024]{2,1,0:T(8,128)(2,1)}) custom-call(s32[48]{0:T(128)} %reshape.43.meta, s32[6,4,256]{2,1,0:T(4,128)} %get-tuple-element.44.code, f32[6,4,256]{2,1,0:T(4,128)} %dynamic-slice_bitcast_fusion.gate, bf16[2,448,2048]{2,1,0:T(8,128)(2,1)} %get-tuple-element.24.early, ...), custom_call_target="tpu_custom_call" | custom-call | flops 7549747200 | bytes 25165824 | tf_op jit(solution)/shard_map/down/pallas_call | solution.py:391
  277.4 57.3 %down.4 = (f32[256,3072]{1,0:T(8,128)}, f32[256,3072]{1,0:T(8,128)}, bf16[2,256,3072]{2,1,0:T(8,128)(2,1)}) custom-call(s32[48]{0:T(128)} %reshape.43.meta, s32[6,4,256]{2,1,0:T(4,128)} %get-tuple-element.44.code, f32[6,4,256]{2,1,0:T(4,128)} %dynamic-slice_bitcast_fusion.gate, bf16[2,448,2048]{2,1,0:T(8,128)(2,1)} %get-tuple-element.24.early, ...), custom_call_target="tpu_custom_call" | custom-call | flops 22649241600 | bytes 75497472 | tf_op jit(solution)/shard_map/down/pallas_call | solution.py:391
  334.6 57.5 %down.5 = (f32[256,3072]{1,0:T(8,128)}, f32[256,3072]{1,0:T(8,128)}, bf16[2,256,3072]{2,1,0:T(8,128)(2,1)}) custom-call(s32[48]{0:T(128)} %reshape.43.meta, s32[6,4,256]{2,1,0:T(4,128)} %get-tuple-element.44.code, f32[6,4,256]{2,1,0:T(4,128)} %dynamic-slice_bitcast_fusion.gate, bf16[2,448,2048]{2,1,0:T(8,128)(2,1)} %get-tuple-element.24.early, ...), custom_call_target="tpu_custom_call" | custom-call | flops 22649241600 | bytes 75497472 | tf_op jit(solution)/shard_map/down/pallas_call | solution.py:391
  392.2 0.5 collective-permute-start.2
  392.7 5.1 %collective-permute-done.4 = bf16[2,256,3072]{2,1,0:T(8,128)(2,1)S(1)} collective-permute-done((bf16[2,256,3072]{2,1,0:T(8,128)(2,1)}, bf16[2,256,3072]{2,1,0:T(8,128)(2,1)S(1)}, u32[]{:S(2)}, u32[]{:S(2)}) %collective-permute-start.4) | collective-permute-done | bytes 3145760 | tf_op jit(solution)/shard_map/ppermute | solution.py:460
  397.9 2.5 fusion
  400.4 1.9 collective-permute-done.2
  402.4 2.5 fusion.4
  405.2 2.0 collective-permute-start.1
  407.1 74.7 %collective-permute-done.1 = bf16[256,1024]{1,0:T(8,128)(2,1)S(1)} collective-permute-done((bf16[256,1024]{1,0:T(8,128)(2,1)S(1)}, bf16[256,1024]{1,0:T(8,128)(2,1)S(1)}, u32[]{:S(2)}, u32[]{:S(2)}) %collective-permute-start.1) | collective-permute-done | bytes 524320 | tf_op jit(solution)/shard_map/ppermute | solution.py:461
  481.8 0.3 fusion.11
  482.2 1.9 fusion.7
  484.1 2.0 maximum_bitcast_fusion
  (28 shorter events, 0.7 us)
Async XLA Ops:
  392.2 5.7 %collective-permute-start.4 = (bf16[2,256,3072]{2,1,0:T(8,128)(2,1)}, bf16[2,256,3072]{2,1,0:T(8,128)(2,1)S(1)}, u32[]{:S(2)}, u32[]{:S(2)}) collective-permute-start(bf16[2,256,3072]{2,1,0:T(8,128)(2,1)} %get-tuple-element.39), channel_id=1, source_target_pairs={{0,1},{1,0},{2,3},{3,2},{4,5},{5,4},{6,7},{7,6}} | collective-permute-start | bytes 9437192 | tf_op jit(solution)/shard_map/ppermute | solution.py:460
  392.2 10.1 %collective-permute-start.2 = (bf16[2,256,3072]{2,1,0:T(8,128)(2,1)}, bf16[2,256,3072]{2,1,0:T(8,128)(2,1)S(1)}, u32[]{:S(2)}, u32[]{:S(2)}) collective-permute-start(bf16[2,256,3072]{2,1,0:T(8,128)(2,1)} %get-tuple-element.34), channel_id=1, source_target_pairs={{0,1},{1,0},{2,3},{3,2},{4,5},{5,4},{6,7},{7,6}} | collective-permute-start | bytes 9437192 | tf_op jit(solution)/shard_map/ppermute | solution.py:460
  392.7 12.3 %collective-permute-start = (bf16[2,256,1024]{2,1,0:T(8,128)(2,1)}, bf16[2,256,1024]{2,1,0:T(8,128)(2,1)S(1)}, u32[]{:S(2)}, u32[]{:S(2)}) collective-permute-start(bf16[2,256,1024]{2,1,0:T(8,128)(2,1)} %get-tuple-element.28), channel_id=1, source_target_pairs={{0,1},{1,0},{2,3},{3,2},{4,5},{5,4},{6,7},{7,6}} | collective-permute-start | bytes 3145736 | tf_op jit(solution)/shard_map/ppermute | solution.py:460
  397.9 7.2 %copy-start.3 = (f32[256,1024]{1,0:T(8,128)S(1)}, f32[256,1024]{1,0:T(8,128)}, u32[]{:S(2)}) copy-start(f32[256,1024]{1,0:T(8,128)} %get-tuple-element.29) | copy-start | bytes 3145732
  397.9 83.9 %slice-start = ((s8[7340032]{0:T(1024)(128)(4,1)}), s8[4194304]{0:T(1024)(128)(4,1)S(1)}, s32[]{:S(2)}) async-start(s8[7340032]{0:T(1024)(128)(4,1)} %bitcast.61), calls=%async_computation | async-start | bytes 8388608
  400.4 81.8 %collective-permute-start.5 = (bf16[256,3072]{1,0:T(8,128)(2,1)S(1)}, bf16[256,3072]{1,0:T(8,128)(2,1)S(1)}, u32[]{:S(2)}, u32[]{:S(2)}) collective-permute-start(bf16[256,3072]{1,0:T(8,128)(2,1)S(1)} %fusion), channel_id=1, source_target_pairs={{0,2},{1,3},{2,0},{3,1},{4,6},{5,7},{6,4},{7,5}} | collective-permute-start | bytes 4718600 | tf_op jit(solution)/shard_map/ppermute | solution.py:461
  402.4 79.4 %slice-start.1 = ((s8[7340032]{0:T(1024)(128)(4,1)}), s8[3145728]{0:T(1024)(128)(4,1)S(1)}, s32[]{:S(2)}) async-start(s8[7340032]{0:T(1024)(128)(4,1)} %bitcast.61), calls=%async_computation.1 | async-start | bytes 6291456
  402.4 79.4 %copy-start.2 = (f32[256,1024]{1,0:T(8,128)S(1)}, f32[256,1024]{1,0:T(8,128)}, u32[]{:S(2)}) copy-start(f32[256,1024]{1,0:T(8,128)} %get-tuple-element.27) | copy-start | bytes 3145732
  402.4 79.8 %copy-start.1 = (f32[256,3072]{1,0:T(8,128)S(1)}, f32[256,3072]{1,0:T(8,128)}, u32[]{:S(2)}) copy-start(f32[256,3072]{1,0:T(8,128)} %get-tuple-element.38) | copy-start | bytes 9437188
  404.9 77.3 %copy-start = (f32[256,3072]{1,0:T(8,128)S(1)}, f32[256,3072]{1,0:T(8,128)}, u32[]{:S(2)}) copy-start(f32[256,3072]{1,0:T(8,128)} %get-tuple-element.33) | copy-start | bytes 9437188
  404.9 77.3 %collective-permute-start.3 = (bf16[256,3072]{1,0:T(8,128)(2,1)S(1)}, bf16[256,3072]{1,0:T(8,128)(2,1)S(1)}, u32[]{:S(2)}, u32[]{:S(2)}) collective-permute-start(bf16[256,3072]{1,0:T(8,128)(2,1)S(1)} %fusion.4), channel_id=1, source_target_pairs={{0,2},{1,3},{2,0},{3,1},{4,6},{5,7},{6,4},{7,5}} | collective-permute-start | bytes 4718600 | tf_op jit(solution)/shard_map/ppermute | solution.py:461
  405.2 76.6 %collective-permute-start.1 = (bf16[256,1024]{1,0:T(8,128)(2,1)S(1)}, bf16[256,1024]{1,0:T(8,128)(2,1)S(1)}, u32[]{:S(2)}, u32[]{:S(2)}) collective-permute-start(bf16[256,1024]{1,0:T(8,128)(2,1)S(1)} %fusion.8), channel_id=1, source_target_pairs={{0,2},{1,3},{2,0},{3,1},{4,6},{5,7},{6,4},{7,5}} | collective-permute-start | bytes 1572872 | tf_op jit(solution)/shard_map/ppermute | solution.py:461

commit v3 on v2

--- a/solution.py
+++ b/solution.py
@@ -7,11 +7,8 @@
 from jax.experimental.pallas import tpu as pltpu
 from jax.sharding import PartitionSpec as P
 
-SAME = [(0, 1), (1, 0), (2, 3), (3, 2)]
-CROSS = [(0, 2), (1, 3), (2, 0), (3, 1)]
 STEP = 112
 EARLY = 2
-CHUNKS = (1024, 3072, 3072)
 VMEM = 63 * 2**20
 KB = 1024
 F32, BF16 = jnp.float32, jnp.bfloat16
@@ -268,7 +265,7 @@
     )(x, table, w_gate, w_up, s_gate, s_up, s_down)
 
 
-def up_kernel(block, meta, code, x0, x1, wg, wu, h_out, z):
+def up_kernel(block, meta, code, x0, x1, wg, wu, h_out, z, packed):
     depth = x0.shape[1]
     e, n = pl.program_id(0), pl.program_id(1)
     at_meta = (e + EARLY) * 8
@@ -293,6 +290,10 @@
         z[pl.ds(total, STEP), :] = jnp.zeros((STEP, depth), BF16)
 
     size = (total + STEP - 1) // STEP
+    @pl.when(size == 0)
+    def _():
+        h_out[...] = jnp.zeros_like(h_out)
+
     for v in range(1, 5):
 
         @pl.when(size == v)
@@ -300,7 +301,11 @@
             m = v * STEP
             g = dot(z[:m, :], wg[0])
             u = dot(z[:m, :], wu[0])
-            h_out[0, :m, :] = (silu(g) * u).astype(BF16)
+            packed[:m, :] = (silu(g) * u).astype(BF16)
+            packed[m : m + STEP, :] = jnp.zeros((STEP, block), BF16)
+            for k in range(4):
+                at = pl.multiple_of(meta[at_meta + k], 16)
+                h_out[0, k * STEP : (k + 1) * STEP, :] = packed[pl.ds(at, STEP), :]
 
 
 def up(meta, code, x0, x1, w_gate, w_up, block):
@@ -321,7 +326,10 @@
                 weight,
             ],
             out_specs=pl.BlockSpec((1, 4 * STEP, block), lambda e, n, m: (e, 0, n)),
-            scratch_shapes=[pltpu.VMEM((5 * STEP, depth), BF16)],
+            scratch_shapes=[
+                pltpu.VMEM((5 * STEP, depth), BF16),
+                pltpu.VMEM((5 * STEP, block), BF16),
+            ],
         ),
         out_shape=jax.ShapeDtypeStruct((late, 4 * STEP, ff), BF16),
         compiler_params=pltpu.CompilerParams(
@@ -336,19 +344,46 @@
     )(meta, code, x0, x1, w_gate, w_up)
 
 
-def down_kernel(experts, meta, code, gate, early, late, wd, own, far, near, h, wt, tmp, stack, sem):
-    first = pl.program_id(0) == 0
+def finish_kernel(
+    chunks, code, gate, early, late, wd, shared, y,
+    h, wt, stack, own, far, near, near_got, out, out_got,
+    sem, near_send, near_recv, out_send, out_recv,
+):
+    experts, block = wd.shape[0], wd.shape[2]
+    i = pl.program_id(0)
+    me = lax.axis_index("ep")
+    partner, across = me + 1 - 2 * lax.rem(me, 2), lax.rem(me + 2, 4)
+
+    def remote(src, dst, send, recv, peer):
+        return pltpu.make_async_remote_copy(
+            src, dst, send, recv, device_id={"ep": peer}, device_id_type=pl.DeviceIdType.MESH
+        )
+
+    def to_partner(j):
+        return remote(
+            near.at[lax.rem(j, 2)], near_got.at[j], near_send.at[lax.rem(j, 2)], near_recv.at[j],
+            partner,
+        )
+
+    def to_across(j):
+        return remote(
+            out.at[lax.rem(j, 2)], out_got.at[j], out_send.at[lax.rem(j, 2)], out_recv.at[j],
+            across,
+        )
 
     def load(e):
-        if e < EARLY:
-            return pltpu.make_async_copy(early.at[e], h.at[e], sem.at[e])
-        return pltpu.make_async_copy(late.at[e - EARLY], h.at[e], sem.at[e])
-
-    @pl.when(first)
-    def _():
+        src = early.at[e] if e < EARLY else late.at[e - EARLY]
+        return pltpu.make_async_copy(src, h.at[e], sem.at[e])
+
+    @pl.when(i == 0)
+    def _():
+        barrier = pltpu.get_barrier_semaphore()
+        for peer in (partner, across):
+            pl.semaphore_signal(
+                barrier, inc=1, device_id={"ep": peer}, device_id_type=pl.DeviceIdType.MESH
+            )
         for e in range(experts):
             load(e).start()
-        tmp[...] = jnp.zeros_like(tmp)
         stack[...] = jnp.zeros_like(stack)
         rows = lax.broadcasted_iota(jnp.int32, (STEP, 256), 0)
         for k in range(4):
@@ -360,74 +395,100 @@
             wt[k] = jnp.concatenate(parts, 0).T.astype(BF16)
         for e in range(experts):
             load(e).wait()
-
-    @pl.loop(0, experts)
-    def _(e):
-        total = meta[e * 8 + 4]
-        size = (total + STEP - 1) // STEP
-        for v in range(1, 5):
-
-            @pl.when(size == v)
-            def _(v=v):
-                m = v * STEP
-                tmp[:m, :] = dot(h[e, :m, :], wd[e]).astype(BF16)
-
-        to = pl.ds(pl.multiple_of(e * STEP, STEP), STEP)
-        for k in range(4):
-            at = pl.multiple_of(meta[e * 8 + k], 16)
-            stack[k, to, :] = tmp[pl.ds(at, STEP), :]
-
-    near[0] = dot(wt[1], stack[1]).astype(BF16)
-    near[1] = dot(wt[3], stack[3]).astype(BF16)
-    far[...] = dot(wt[2], stack[2])
-    own[...] = dot(wt[0], stack[0])
-
-
-def down(meta, code, gate, early, late, w_down, start, columns, block):
-    experts, ff, _ = w_down.shape
+        pl.semaphore_wait(barrier, 2)
+
+    @pl.when((i >= 1) & (i <= chunks))
+    def _():
+        j = i - 1
+
+        @pl.when(j >= 2)
+        def _():
+            to_across(j - 2).wait_send()
+
+        to_partner(j).wait_recv()
+        out[lax.rem(j, 2)] = (far[...] + near_got[j, 1].astype(F32)).astype(BF16)
+
+    @pl.when(i >= 2)
+    def _():
+        j = i - 2
+        to_across(j).wait_recv()
+        total = own[lax.rem(j, 3)] + near_got[j, 0].astype(F32) + out_got[j].astype(F32)
+        y[...] = (total + shared[...]).astype(BF16)
+
+    @pl.when((i >= 1) & (i <= chunks))
+    def _():
+        to_across(i - 1).start()
+
+    @pl.when(i < chunks)
+    def _():
+        for e in range(experts):
+            made = dot(h[e], wd[e]).astype(BF16)
+            for k in range(4):
+                stack[k, e * STEP : (e + 1) * STEP, :] = made[k * STEP : (k + 1) * STEP, :]
+
+        @pl.when(i >= 2)
+        def _():
+            to_partner(i - 2).wait_send()
+
+        slot = lax.rem(i, 2)
+        near[slot, 1] = dot(wt[3], stack[3]).astype(BF16)
+        near[slot, 0] = dot(wt[1], stack[1]).astype(BF16)
+        far[...] = dot(wt[2], stack[2])
+        to_partner(i).start()
+        own[lax.rem(i, 3)] = dot(wt[0], stack[0])
+
+    @pl.when(i == chunks + 1)
+    def _():
+        for j in (chunks - 2, chunks - 1):
+            to_partner(j).wait_send()
+            to_across(j).wait_send()
+
+
+def finish(code, gate, early, late, w_down, shared, block):
+    experts, ff, d = w_down.shape
+    chunks = d // block
     once = pl.Buffered(1)
-    small = pl.BlockSpec((experts, 4, 256), lambda n, m: (0, 0, 0), pipeline_mode=once)
+    small = pl.BlockSpec((experts, 4, 256), lambda i: (0, 0, 0), pipeline_mode=once)
+    result = pl.BlockSpec((256, block), lambda i: (0, jnp.maximum(i - 2, 0)))
     depth = -(-experts * STEP // 256) * 256
+    dma = pltpu.SemaphoreType.DMA
     return pl.pallas_call(
-        functools.partial(down_kernel, experts),
-        grid_spec=pltpu.PrefetchScalarGridSpec(
-            num_scalar_prefetch=1,
-            grid=(columns // block,),
-            in_specs=[
-                small,
-                small,
-                pl.BlockSpec(memory_space=pl.ANY),
-                pl.BlockSpec(memory_space=pl.ANY),
-                pl.BlockSpec((experts, ff, block), lambda n, m: (0, 0, n + start // block)),
-            ],
-            out_specs=[
-                pl.BlockSpec((256, block), lambda n, m: (0, n)),
-                pl.BlockSpec((256, block), lambda n, m: (0, n)),
-                pl.BlockSpec((2, 256, block), lambda n, m: (0, 0, n)),
-            ],
-            scratch_shapes=[
-                pltpu.VMEM((experts, 4 * STEP, ff), BF16),
-                pltpu.VMEM((4, 256, depth), BF16),
-                pltpu.VMEM((5 * STEP, block), BF16),
-                pltpu.VMEM((4, depth, block), BF16),
-                pltpu.SemaphoreType.DMA((experts,)),
-            ],
+        functools.partial(finish_kernel, chunks),
+        grid=(chunks + 2,),
+        in_specs=[
+            small,
+            small,
+            pl.BlockSpec(memory_space=pl.ANY),
+            pl.BlockSpec(memory_space=pl.ANY),
+            pl.BlockSpec((experts, ff, block), lambda i: (0, 0, jnp.minimum(i, chunks - 1))),
+            result,
+        ],
+        out_specs=result,
+        scratch_shapes=[
+            pltpu.VMEM((experts, 4 * STEP, ff), BF16),
+            pltpu.VMEM((4, 256, depth), BF16),
+            pltpu.VMEM((4, depth, block), BF16),
+            pltpu.VMEM((3, 256, block), F32),
+            pltpu.VMEM((256, block), F32),
+            pltpu.VMEM((2, 2, 256, block), BF16),
+            pltpu.VMEM((chunks, 2, 256, block), BF16),
+            pltpu.VMEM((2, 256, block), BF16),
+            pltpu.VMEM((chunks, 256, block), BF16),
+            dma((experts,)),
+            dma((2,)),
+            dma((chunks,)),
+            dma((2,)),
+            dma((chunks,)),
+        ],
+        out_shape=jax.ShapeDtypeStruct((256, d), BF16),
+        compiler_params=pltpu.CompilerParams(
+            collective_id=1,
+            has_side_effects=True,
+            vmem_limit_bytes=VMEM,
+            dimension_semantics=("arbitrary",),
         ),
-        out_shape=[
-            jax.ShapeDtypeStruct((256, columns), F32),
-            jax.ShapeDtypeStruct((256, columns), F32),
-            jax.ShapeDtypeStruct((2, 256, columns), BF16),
-        ],
-        compiler_params=pltpu.CompilerParams(
-            vmem_limit_bytes=VMEM, dimension_semantics=("arbitrary",)
-        ),
-        cost_estimate=pl.CostEstimate(
-            flops=experts * 300 * columns * ff * 2,
-            bytes_accessed=experts * columns * ff * 2,
-            transcendentals=0,
-        ),
-        name="down",
-    )(meta, code, gate, early, late, w_down)
+        name="finish",
+    )(code, gate, early, late, w_down, shared)
 
 
 def layer(x, expert, slot, gate, w_gate, w_up, w_down, s_gate, s_up, s_down):
@@ -436,34 +497,19 @@
     x, expert, slot, gate = x[0, 0], expert[0, 0], slot[0, 0], gate[0, 0]
     tokens, top = expert.shape
     slots = 5 * tokens * top // (4 * experts)
-    same = functools.partial(lax.ppermute, axis_name="ep", perm=SAME)
-    cross = functools.partial(lax.ppermute, axis_name="ep", perm=CROSS)
-
     table = tables(expert, slot, gate, experts, slots)
     xs, table, early, shared = arrive(x, table, w_gate, w_up, s_gate, s_up, s_down)
     table = lax.dynamic_slice_in_dim(table, lax.axis_index("ep") * local, local, 2)
     code = table[:, 0].transpose(1, 0, 2).astype(jnp.int32)
     weight = table[:, 1].transpose(1, 0, 2)
     used = (jnp.max(code, -1) + 16) // 16 * 16
-    used = jnp.where(jnp.arange(local)[:, None] < EARLY, STEP, used)
     starts = [jnp.zeros_like(used[:, 0])]
     for k in range(4):
         starts.append(starts[-1] + used[:, k])
     meta = jnp.stack(starts + starts[:3], 1).reshape(-1)
 
     late = up(meta, code, x, xs, w_gate, w_up, 512)
-
-    pieces, start = [], 0
-    for columns in CHUNKS:
-        own, far, near = down(meta, code, weight, early, late, w_down, start, columns, 512)
-        meta, own = lax.optimization_barrier((meta, own))
-        near = same(near)
-        far = cross((far + near[1].astype(F32)).astype(BF16))
-        total = own + near[0].astype(F32) + far.astype(F32)
-        total = total + shared[:, start : start + columns]
-        pieces.append(total.astype(BF16))
-        start += columns
-    return jnp.concatenate(pieces, 1)[None, None]
+    return finish(code, weight, early, late, w_down, shared, 512)[None, None]
 
 
 def solution(mesh):

time: 493 us -> 396 us (0.80)
  waiting for transfers between devices: 81.7 us -> 0 us
  other arithmetic: 13.9 us -> 4.39 us
    ppermute x6 -> x0, waiting for transfers between devices: 81.7 us -> none  [the longest x3 74.7 us: layer(): far = cross((far + near[1].astype(F32)).astype(BF16))]
    pallas_call x1, Pallas kernels: 121 us -> 107 us  [up(): pl.pallas_call(functools.partial(up_kernel, block), grid_spec=pltpu.Prefe...]
    pallas_call x3 -> x1, Pallas kernels: 143 us -> 155 us  [finish(): pl.pallas_call(functools.partial(finish_kernel, chunks), grid=(chunks + 2...]
    convert_element_type x5 -> x0, other arithmetic: 7.44 us -> none  [the longest x3 5.19 us: layer(): far = cross((far + near[1].astype(F32)).astype(BF16))]
  transfers between devices with their start and end apart: 6 -> 0, of which waited for: 3 -> 0; matrix products, arithmetic and copies ran while one was open for 1% -> 0% of each run, Pallas kernels for 0% -> 0%
where the time goes in v3:
time: 396 us; the launch traced here: 394 us
  Pallas kernels  383 us (97%)
  local copies, waits for them, and re-layouts  6.53 us (2%)
  other arithmetic  4.39 us (1%)
    pallas_call x1, Pallas kernels, finish(): pl.pallas_call(functools.partial(finish_kernel, chunks), grid=(chunks + 2...  155 us
    pallas_call x1, Pallas kernels, arrive(): pl.pallas_call(functools.partial(arrive_kernel, local), in_specs=[vmem] *...  121 us
    pallas_call x1, Pallas kernels, up(): pl.pallas_call(functools.partial(up_kernel, block), grid_spec=pltpu.Prefe...  107 us

profile of v3, /device:TPU:0, one launch (start us, length us, event | category | flops | bytes accessed | tf_op | source)
XLA Modules:
  0.0 393.6 jit_solution(9551345045804589255)
XLA Ops:
  0.0 0.7 compare_bitcast_fusion
  0.7 0.7 add_bitcast_fusion
  1.4 0.8 select_reduce_fusion.1
  2.2 0.8 select_reduce_fusion
  3.0 0.6 pad_maximum_fusion.table
  3.6 120.8 %arrive.1 = (bf16[3,256,7168]{2,1,0:T(8,128)(2,1)}, f32[4,2,24,256]{3,2,1,0:T(8,128)}, bf16[2,448,2048]{2,1,0:T(8,128)(2,1)}, f32[256,7168]{1,0:T(8,128)}) custom-call(bf16[256,7168]{1,0:T(8,128)(2,1)} %bitcast.28, f32[2,24,256]{2,1,0:T(8,128)} %pad_maximum_fusion.table, bf16[6,7168,2048]{2,1,0:T(8,128)(2,1)} %wg.1, bf16[6,7168,2048]{2,1,0:T(8,128)(2,1)} %wu.1, ...), custom_call_target="tpu_custom_call" | custom-call | tf_op jit(solution)/shard_map/arrive/pallas_call | solution.py:237
  124.5 1.1 copy.12
  125.5 0.6 dynamic-slice_bitcast_fusion.gate
  126.1 0.6 fusion.5
  126.8 0.1 slice_add_fusion
  126.8 0.1 slice_add_fusion.1
  126.9 0.1 stack.16
  127.0 0.7 reshape.26.meta
  127.7 107.0 %up.1.late = bf16[4,448,2048]{2,1,0:T(8,128)(2,1)} custom-call(s32[48]{0:T(128)} %reshape.26.meta, s32[6,4,256]{2,1,0:T(4,128)} %get-tuple-element.16.code, bf16[256,7168]{1,0:T(8,128)(2,1)} %bitcast.29, bf16[3,256,7168]{2,1,0:T(8,128)(2,1)} %get-tuple-element.11.x1, bf16[6,7168,2048]{2,1,0:T(8,128)(2,1)} %wg.1, bf16[6,7168,2048]{2,1,0:T(8,128)(2,1)} %wu.1), custom_call_target="tpu_custom_call" | custom-call | flops 70464307200 | bytes 234881024 | tf_op jit(solution)/shard_map/up/pallas_call | solution.py:316
  234.7 154.8 %finish.1 = bf16[256,7168]{1,0:T(8,128)(2,1)} custom-call(s32[6,4,256]{2,1,0:T(4,128)} %get-tuple-element.16.code, f32[6,4,256]{2,1,0:T(4,128)} %dynamic-slice_bitcast_fusion.gate, bf16[2,448,2048]{2,1,0:T(8,128)(2,1)} %get-tuple-element.10.early, bf16[4,448,2048]{2,1,0:T(8,128)(2,1)} %up.1.late, bf16[6,2048,7168]{2,1,0:T(8,128)(2,1)} %wd.1, ...), custom_call_target="tpu_custom_call" | custom-call | tf_op jit(solution)/shard_map/finish/pallas_call | solution.py:455
  389.4 4.1 %copy.14 = bf16[1,1,256,7168]{3,2,1,0:T(8,128)(2,1)} copy(bf16[1,1,256,7168]{3,2,1,0:T(8,128)(2,1)} %bitcast.30) | data formatting | bytes 7340032
  (3 shorter events, 0.0 us)

commit v4 on v3

--- a/solution.py
+++ b/solution.py
@@ -32,12 +32,12 @@
 
 def arrive_kernel(
     local, x, table, w_gate, w_up, s_gate, s_up, s_down,
-    xs, tabs, h, shared,
-    got, tab, ring, ring2, acc_s, acc, z, hidden, stage,
+    xs, codes, gates, h, shared,
+    got, tab, ring, ring2, acc, z, hidden, stage,
     ring_sem, ring2_sem, stage_sem, cross_send, cross_recv, pass_send, pass_recv,
     own_send, own_recv, tab_send, tab_recv, out_sem,
 ):
-    d, ff = x.shape[1], s_gate.shape[1]
+    (tokens, d), ff = x.shape, s_gate.shape[1]
     chunks = d // KB
     me = lax.axis_index("ep")
     partner, across = me + 1 - 2 * lax.rem(me, 2), lax.rem(me + 2, 4)
@@ -109,8 +109,10 @@
 
     wide = ring2.shape[2]
 
+    deep = ring2.shape[0]
+
     def down_tile(n):
-        slot = lax.rem(n, 2)
+        slot = lax.rem(n, deep)
         c = pl.ds(pl.multiple_of(n * wide, wide), wide)
         return pltpu.make_async_copy(s_down.at[:, c], ring2.at[slot], ring2_sem.at[slot])
 
@@ -129,10 +131,8 @@
     own.start()
     for j in range(slots):
         fetch(jnp.int32(j))
-    down_tile(0).start()
-    down_tile(1).start()
-
-    acc_s[...] = jnp.zeros_like(acc_s)
+    for n in range(deep):
+        down_tile(jnp.int32(n)).start()
 
     @pl.loop(0, n_shared)
     def _(j):
@@ -141,59 +141,62 @@
         side = lax.rem(j, 2)
         for n in range(ff // 512):
             c = slice(n * 512, n * 512 + 512)
-            acc_s[side, :, c] += dot(a, ring[slot, :, c])
+            old = jnp.where(j < 2, 0.0, acc[side, :tokens, c])
+            acc[side, :tokens, c] = old + dot(a, ring[slot, :, c])
         fetch(j + slots)
 
     for n in range(ff // 512):
         c = slice(n * 512, n * 512 + 512)
-        hidden[:, c] = (silu(acc_s[0, :, c]) * acc_s[1, :, c]).astype(BF16)
-
-    n_down = d // wide
-
-    @pl.loop(0, n_down)
-    def _(n):
-        down_tile(n).wait()
-
-        @pl.when(n >= 2)
-        def _():
-            put(n - 2).wait()
-
-        slot = lax.rem(n, 2)
-        stage[slot] = dot(hidden[...], ring2[slot])
-
-        @pl.when(n + 2 < n_down)
-        def _():
-            down_tile(n + 2).start()
-
-        put(n).start()
-
-    put(n_down - 2).wait()
-    put(n_down - 1).wait()
-
-    for copy in tab_copies:
-        copy.wait()
-    tabs[0] = table[...]
-    for i in range(3):
-        tabs[1 + i] = tab[i]
-    own.wait()
-
-    acc[...] = jnp.zeros_like(acc)
-    rows = lax.broadcasted_iota(jnp.int32, (STEP, 256), 0).astype(F32)
-
-    @pl.loop(0, chunks)
-    def _(k):
-        c = columns(k)
+        hidden[:, c] = (silu(acc[0, :tokens, c]) * acc[1, :tokens, c]).astype(BF16)
+
+    def pass_on(k):
         cross(k).wait_recv()
         onward(k).start()
         keep(0, k).start()
         keep(1, k).start()
 
+    own.wait()
+    pass_on(jnp.int32(0))
+    n_down = d // wide
+
+    @pl.loop(0, n_down)
+    def _(n):
+        down_tile(n).wait()
+
+        @pl.when(n >= 2)
+        def _():
+            put(n - 2).wait()
+
+        slot = lax.rem(n, 2)
+        stage[slot] = dot(hidden[...], ring2[lax.rem(n, deep)])
+
+        @pl.when(n + deep < n_down)
+        def _():
+            down_tile(n + deep).start()
+
+        put(n).start()
+
+    put(n_down - 2).wait()
+    put(n_down - 1).wait()
+
+    for copy in tab_copies:
+        copy.wait()
+    for e in range(local):
+        for i in range(4):
+            t = table if i == 0 else tab.at[i - 1]
+            row = pl.ds(me * local + e, 1)
+            codes[e, i : i + 1, :] = t[0, row, :]
+            gates[e, i : i + 1, :] = t[1, row, :]
+
+    rows = lax.broadcasted_iota(jnp.int32, (STEP, 256), 0).astype(F32)
+
+    @pl.loop(0, chunks)
+    def _(k):
+        c = columns(k)
         def picked(i, a):
             parts = []
             for e in range(EARLY):
-                t = table if i == 0 else tab.at[i - 1]
-                code = t[0, pl.ds(me * local + e, 1), :]
-                parts.append((rows == code).astype(BF16))
+                parts.append((rows == codes[e, i : i + 1, :]).astype(BF16))
             z_i = dot(jnp.concatenate(parts, 0), a).astype(BF16)
             for e in range(EARLY):
                 z[e, i * STEP : (i + 1) * STEP, :] = z_i[e * STEP : (e + 1) * STEP, :]
@@ -209,9 +212,15 @@
         def _(q):
             j = n_shared + 2 * EARLY * k + q
             slot = ready(j)
+
+            @pl.when((q == EARLY) & (k + 1 < chunks))
+            def _():
+                pass_on(k + 1)
+
             for n in range(ff // 512):
                 cc = slice(n * 512, n * 512 + 512)
-                acc[q, :, cc] += dot(z[q // 2], ring[slot, :, cc])
+                old = jnp.where(k == 0, 0.0, acc[q, :, cc])
+                acc[q, :, cc] = old + dot(z[q // 2], ring[slot, :, cc])
             fetch(j + slots)
 
     for e in range(EARLY):
@@ -237,10 +246,11 @@
     return pl.pallas_call(
         functools.partial(arrive_kernel, local),
         in_specs=[vmem] * 2 + [hbm] * 5,
-        out_specs=[hbm, vmem, vmem, hbm],
+        out_specs=[hbm, vmem, vmem, vmem, hbm],
         out_shape=[
             jax.ShapeDtypeStruct((3, tokens, d), BF16),
-            jax.ShapeDtypeStruct((4, *table.shape), F32),
+            jax.ShapeDtypeStruct((local, 4, tokens), F32),
+            jax.ShapeDtypeStruct((local, 4, tokens), F32),
             jax.ShapeDtypeStruct((EARLY, 4 * STEP, ff), BF16),
             jax.ShapeDtypeStruct((tokens, d), F32),
         ],
@@ -248,13 +258,12 @@
             pltpu.VMEM((3, tokens, d), BF16),
             pltpu.VMEM((3, *table.shape), F32),
             pltpu.VMEM((3, KB, ff), BF16),
-            pltpu.VMEM((2, ff, 512), BF16),
-            pltpu.VMEM((2, tokens, ff), F32),
+            pltpu.VMEM((4, ff, 512), BF16),
             pltpu.VMEM((2 * EARLY, 4 * STEP, ff), F32),
             pltpu.VMEM((EARLY, 4 * STEP, KB), BF16),
             pltpu.VMEM((tokens, ff), BF16),
             pltpu.VMEM((2, tokens, 512), F32),
-            dma((3,)), dma((2,)), dma((2,)),
+            dma((3,)), dma((4,)), dma((2,)),
             dma((chunks,)), dma((chunks,)), dma((chunks,)), dma((chunks,)),
             dma, dma, dma((3,)), dma((3,)), dma((3, chunks)),
         ],
@@ -265,7 +274,7 @@
     )(x, table, w_gate, w_up, s_gate, s_up, s_down)
 
 
-def up_kernel(block, meta, code, x0, x1, wg, wu, h_out, z, packed):
+def up_kernel(block, meta, code, x0, x1, wg, wu, h_out, z, packed, gated):
     depth = x0.shape[1]
     e, n = pl.program_id(0), pl.program_id(1)
     at_meta = (e + EARLY) * 8
@@ -273,12 +282,12 @@
 
     @pl.when(n == 0)
     def _():
-        rows = lax.broadcasted_iota(jnp.int32, (STEP, 256), 0)
+        rows = lax.broadcasted_iota(jnp.int32, (STEP, 256), 0).astype(F32)
         picks = [(rows == code[0, k : k + 1, :]).astype(BF16) for k in range(4)]
 
-        @pl.loop(0, depth // 1024)
+        @pl.loop(0, depth // 1792)
         def _(c):
-            cols = pl.ds(pl.multiple_of(c * 1024, 1024), 1024)
+            cols = pl.ds(pl.multiple_of(c * 1792, 256), 1792)
             parts = [
                 dot(picks[k], x0[:, cols] if k == 0 else x1[k - 1, :, cols]).astype(BF16)
                 for k in range(4)
@@ -299,9 +308,9 @@
         @pl.when(size == v)
         def _(v=v):
             m = v * STEP
-            g = dot(z[:m, :], wg[0])
+            gated[:m, :] = silu(dot(z[:m, :], wg[0]))
             u = dot(z[:m, :], wu[0])
-            packed[:m, :] = (silu(g) * u).astype(BF16)
+            packed[:m, :] = (gated[:m, :] * u).astype(BF16)
             packed[m : m + STEP, :] = jnp.zeros((STEP, block), BF16)
             for k in range(4):
                 at = pl.multiple_of(meta[at_meta + k], 16)
@@ -329,6 +338,7 @@
             scratch_shapes=[
                 pltpu.VMEM((5 * STEP, depth), BF16),
                 pltpu.VMEM((5 * STEP, block), BF16),
+                pltpu.VMEM((4 * STEP, block), F32),
             ],
         ),
         out_shape=jax.ShapeDtypeStruct((late, 4 * STEP, ff), BF16),
@@ -385,7 +395,7 @@
         for e in range(experts):
             load(e).start()
         stack[...] = jnp.zeros_like(stack)
-        rows = lax.broadcasted_iota(jnp.int32, (STEP, 256), 0)
+        rows = lax.broadcasted_iota(jnp.int32, (STEP, 256), 0).astype(F32)
         for k in range(4):
             parts = [
                 jnp.where(rows == code[e, k : k + 1, :], gate[e, k : k + 1, :], 0.0)
@@ -393,9 +403,28 @@
             ]
             parts.append(jnp.zeros((stack.shape[1] - experts * STEP, 256), F32))
             wt[k] = jnp.concatenate(parts, 0).T.astype(BF16)
-        for e in range(experts):
+        for e in range(experts // 2):
             load(e).wait()
         pl.semaphore_wait(barrier, 2)
+
+    @pl.when(i >= 3)
+    def _():
+        j = i - 3
+        to_across(j).wait_recv()
+        total = own[lax.rem(j, 4)] + near_got[j, 0].astype(F32) + out_got[j].astype(F32)
+        y[...] = (total + shared[...]).astype(BF16)
+
+    def make(e):
+        made = dot(h[e], wd[e]).astype(BF16)
+        for k in range(4):
+            stack[k, e * STEP : (e + 1) * STEP, :] = made[k * STEP : (k + 1) * STEP, :]
+
+    half = experts // 2
+
+    @pl.when(i < chunks)
+    def _():
+        for e in range(half):
+            make(e)
 
     @pl.when((i >= 1) & (i <= chunks))
     def _():
@@ -407,24 +436,17 @@
 
         to_partner(j).wait_recv()
         out[lax.rem(j, 2)] = (far[...] + near_got[j, 1].astype(F32)).astype(BF16)
-
-    @pl.when(i >= 2)
-    def _():
-        j = i - 2
-        to_across(j).wait_recv()
-        total = own[lax.rem(j, 3)] + near_got[j, 0].astype(F32) + out_got[j].astype(F32)
-        y[...] = (total + shared[...]).astype(BF16)
-
-    @pl.when((i >= 1) & (i <= chunks))
-    def _():
-        to_across(i - 1).start()
+        to_across(j).start()
+
+    @pl.when(i == 0)
+    def _():
+        for e in range(half, experts):
+            load(e).wait()
 
     @pl.when(i < chunks)
     def _():
-        for e in range(experts):
-            made = dot(h[e], wd[e]).astype(BF16)
-            for k in range(4):
-                stack[k, e * STEP : (e + 1) * STEP, :] = made[k * STEP : (k + 1) * STEP, :]
+        for e in range(half, experts):
+            make(e)
 
         @pl.when(i >= 2)
         def _():
@@ -435,9 +457,9 @@
         near[slot, 0] = dot(wt[1], stack[1]).astype(BF16)
         far[...] = dot(wt[2], stack[2])
         to_partner(i).start()
-        own[lax.rem(i, 3)] = dot(wt[0], stack[0])
-
-    @pl.when(i == chunks + 1)
+        own[lax.rem(i, 4)] = dot(wt[0], stack[0])
+
+    @pl.when(i == chunks + 2)
     def _():
         for j in (chunks - 2, chunks - 1):
             to_partner(j).wait_send()
@@ -449,12 +471,12 @@
     chunks = d // block
     once = pl.Buffered(1)
     small = pl.BlockSpec((experts, 4, 256), lambda i: (0, 0, 0), pipeline_mode=once)
-    result = pl.BlockSpec((256, block), lambda i: (0, jnp.maximum(i - 2, 0)))
+    result = pl.BlockSpec((256, block), lambda i: (0, jnp.maximum(i - 3, 0)))
     depth = -(-experts * STEP // 256) * 256
     dma = pltpu.SemaphoreType.DMA
     return pl.pallas_call(
         functools.partial(finish_kernel, chunks),
-        grid=(chunks + 2,),
+        grid=(chunks + 3,),
         in_specs=[
             small,
             small,
@@ -468,7 +490,7 @@
             pltpu.VMEM((experts, 4 * STEP, ff), BF16),
             pltpu.VMEM((4, 256, depth), BF16),
             pltpu.VMEM((4, depth, block), BF16),
-            pltpu.VMEM((3, 256, block), F32),
+            pltpu.VMEM((4, 256, block), F32),
             pltpu.VMEM((256, block), F32),
             pltpu.VMEM((2, 2, 256, block), BF16),
             pltpu.VMEM((chunks, 2, 256, block), BF16),
@@ -498,11 +520,8 @@
     tokens, top = expert.shape
     slots = 5 * tokens * top // (4 * experts)
     table = tables(expert, slot, gate, experts, slots)
-    xs, table, early, shared = arrive(x, table, w_gate, w_up, s_gate, s_up, s_down)
-    table = lax.dynamic_slice_in_dim(table, lax.axis_index("ep") * local, local, 2)
-    code = table[:, 0].transpose(1, 0, 2).astype(jnp.int32)
-    weight = table[:, 1].transpose(1, 0, 2)
-    used = (jnp.max(code, -1) + 16) // 16 * 16
+    xs, code, weight, early, shared = arrive(x, table, w_gate, w_up, s_gate, s_up, s_down)
+    used = (jnp.max(code, -1).astype(jnp.int32) + 16) // 16 * 16
     starts = [jnp.zeros_like(used[:, 0])]
     for k in range(4):
         starts.append(starts[-1] + used[:, k])

time: 396 us -> 361 us (0.912); the launches traced: 394 us -> 366 us
  Pallas kernels: 383 us -> 356 us
    pallas_call x1, Pallas kernels: 155 us -> 141 us  [finish(): pl.pallas_call(functools.partial(finish_kernel, chunks), grid=(chunks + 3...]
    pallas_call x1, Pallas kernels: 121 us -> 109 us  [arrive(): pl.pallas_call(functools.partial(arrive_kernel, local), in_specs=[vmem] *...]
where the time goes in v4:
time: 361 us; the launch traced here: 366 us
  Pallas kernels  356 us (99%)
  local copies, waits for them, and re-layouts  4.79 us (1%)
  other arithmetic  4.59 us (1%)
    pallas_call x1, Pallas kernels, finish(): pl.pallas_call(functools.partial(finish_kernel, chunks), grid=(chunks + 3...  141 us
    pallas_call x1, Pallas kernels, arrive(): pl.pallas_call(functools.partial(arrive_kernel, local), in_specs=[vmem] *...  109 us
    pallas_call x1, Pallas kernels, up(): pl.pallas_call(functools.partial(up_kernel, block), grid_spec=pltpu.Prefe...  107 us

profile of v4, /device:TPU:0, one launch (start us, length us, event | category | flops | bytes accessed | tf_op | source)
XLA Modules:
  0.0 365.8 jit_solution(3733489039213461119)
XLA Ops:
  0.0 0.7 compare_bitcast_fusion
  0.7 0.7 add_bitcast_fusion
  1.4 0.8 select_reduce_fusion.1
  2.2 0.8 select_reduce_fusion
  3.0 0.6 pad_maximum_fusion.table
  3.6 108.8 %arrive.1 = (bf16[3,256,7168]{2,1,0:T(8,128)(2,1)}, f32[6,4,256]{2,1,0:T(4,128)}, f32[6,4,256]{2,1,0:T(4,128)}, bf16[2,448,2048]{2,1,0:T(8,128)(2,1)}, f32[256,7168]{1,0:T(8,128)}) custom-call(bf16[256,7168]{1,0:T(8,128)(2,1)} %bitcast.19, f32[2,24,256]{2,1,0:T(8,128)} %pad_maximum_fusion.table, bf16[6,7168,2048]{2,1,0:T(8,128)(2,1)} %wg.1, ...), custom_call_target="tpu_custom_call" | custom-call | tf_op jit(solution)/shard_map/arrive/pallas_call | solution.py:246
  112.5 0.8 reduce_max.9
  113.3 0.1 slice_add_fusion
  113.4 0.1 slice_add_fusion.1
  113.4 0.1 stack.16
  113.5 0.6 reshape.25.meta
  114.1 106.6 %up.1.late = bf16[4,448,2048]{2,1,0:T(8,128)(2,1)} custom-call(s32[48]{0:T(128)} %reshape.25.meta, f32[6,4,256]{2,1,0:T(4,128)} %get-tuple-element.10.code, bf16[256,7168]{1,0:T(8,128)(2,1)} %bitcast.20, bf16[3,256,7168]{2,1,0:T(8,128)(2,1)} %get-tuple-element.13.x1, bf16[6,7168,2048]{2,1,0:T(8,128)(2,1)} %wg.1, bf16[6,7168,2048]{2,1,0:T(8,128)(2,1)} %wu.1), custom_call_target="tpu_custom_call" | custom-call | flops 70464307200 | bytes 234881024 | tf_op jit(solution)/shard_map/up/pallas_call | solution.py:325
  220.8 140.9 %finish.1 = bf16[256,7168]{1,0:T(8,128)(2,1)} custom-call(f32[6,4,256]{2,1,0:T(4,128)} %get-tuple-element.10.code, f32[6,4,256]{2,1,0:T(4,128)} %get-tuple-element.11.gate, bf16[2,448,2048]{2,1,0:T(8,128)(2,1)} %get-tuple-element.12.early, bf16[4,448,2048]{2,1,0:T(8,128)(2,1)} %up.1.late, bf16[6,2048,7168]{2,1,0:T(8,128)(2,1)} %wd.1, ...), custom_call_target="tpu_custom_call" | custom-call | tf_op jit(solution)/shard_map/finish/pallas_call | solution.py:477
  361.7 4.1 %copy.12 = bf16[1,1,256,7168]{3,2,1,0:T(8,128)(2,1)} copy(bf16[1,1,256,7168]{3,2,1,0:T(8,128)(2,1)} %bitcast.21) | data formatting | bytes 7340032
  (3 shorter events, 0.0 us)

commit v5 on v4

--- a/solution.py
+++ b/solution.py
@@ -274,84 +274,147 @@
     )(x, table, w_gate, w_up, s_gate, s_up, s_down)
 
 
-def up_kernel(block, meta, code, x0, x1, wg, wu, h_out, z, packed, gated):
-    depth = x0.shape[1]
-    e, n = pl.program_id(0), pl.program_id(1)
-    at_meta = (e + EARLY) * 8
-    total = pl.multiple_of(meta[at_meta + 4], 16)
-
-    @pl.when(n == 0)
-    def _():
-        rows = lax.broadcasted_iota(jnp.int32, (STEP, 256), 0).astype(F32)
-        picks = [(rows == code[0, k : k + 1, :]).astype(BF16) for k in range(4)]
-
-        @pl.loop(0, depth // 1792)
-        def _(c):
-            cols = pl.ds(pl.multiple_of(c * 1792, 256), 1792)
-            parts = [
-                dot(picks[k], x0[:, cols] if k == 0 else x1[k - 1, :, cols]).astype(BF16)
-                for k in range(4)
-            ]
-            for k in range(4):
-                at = pl.multiple_of(meta[at_meta + k], 16)
-                z[pl.ds(at, STEP), cols] = parts[k]
-
-        z[pl.ds(total, STEP), :] = jnp.zeros((STEP, depth), BF16)
-
-    size = (total + STEP - 1) // STEP
-    @pl.when(size == 0)
-    def _():
-        h_out[...] = jnp.zeros_like(h_out)
-
-    for v in range(1, 5):
-
-        @pl.when(size == v)
-        def _(v=v):
-            m = v * STEP
-            gated[:m, :] = silu(dot(z[:m, :], wg[0]))
-            u = dot(z[:m, :], wu[0])
-            packed[:m, :] = (gated[:m, :] * u).astype(BF16)
-            packed[m : m + STEP, :] = jnp.zeros((STEP, block), BF16)
-            for k in range(4):
-                at = pl.multiple_of(meta[at_meta + k], 16)
-                h_out[0, k * STEP : (k + 1) * STEP, :] = packed[pl.ds(at, STEP), :]
-
-
-def up(meta, code, x0, x1, w_gate, w_up, block):
+def up_kernel(
+    meta, code, x0, xs, w_gate, w_up, h_out,
+    z, part, ring, packed, piece, part_sem, ring_sem, piece_sem,
+):
+    late, depth = code.shape[0] - EARLY, x0.shape[1]
+    slots, block = ring.shape[0], ring.shape[2] // 2
+    n_jobs = late * w_gate.shape[2] // block
+    width = part.shape[3]
+
+    def begin(e, k):
+        return pl.multiple_of(meta[(e + EARLY) * 8 + k], 16)
+
+    def fetches(j):
+        e, slot = lax.rem(j, late) + EARLY, lax.rem(j, slots)
+        c = pl.ds(pl.multiple_of((j // late) * block, block), block)
+        return [
+            pltpu.make_async_copy(
+                w.at[e, :, c], ring.at[slot, :, pl.ds(i * block, block)], ring_sem.at[slot, i]
+            )
+            for i, w in enumerate((w_gate, w_up))
+        ]
+
+    def columns(c):
+        return pl.ds(pl.multiple_of(c * width, width), width)
+
+    def tokens(c):
+        at = lax.rem(c, 2)
+        return [
+            pltpu.make_async_copy(x0.at[:, columns(c)], part.at[at, 0], part_sem.at[at, 0]),
+            pltpu.make_async_copy(
+                xs.at[:, :, columns(c)], part.at[at, pl.ds(1, 3)], part_sem.at[at, 1]
+            ),
+        ]
+
+    for c in range(2):
+        for copy in tokens(jnp.int32(c)):
+            copy.start()
+    for j in range(slots):
+        for copy in fetches(jnp.int32(j)):
+            copy.start()
+
+    rows = lax.broadcasted_iota(jnp.int32, (STEP, 256), 0).astype(F32)
+    picks = [
+        jnp.concatenate(
+            [(rows == code[e + EARLY, k : k + 1, :]).astype(BF16) for e in range(late)], 0
+        )
+        for k in range(4)
+    ]
+
+    @pl.loop(0, depth // width)
+    def _(c):
+        for copy in tokens(c):
+            copy.wait()
+        for e in range(late):
+            at = pl.multiple_of(e * 4 * STEP + begin(e, 4), 16)
+            z[pl.ds(at, STEP), columns(c)] = jnp.zeros((STEP, width), BF16)
+        for k in range(4):
+            got = dot(picks[k], part[lax.rem(c, 2), k]).astype(BF16)
+            for e in range(late):
+                at = pl.multiple_of(e * 4 * STEP + begin(e, k), 16)
+                z[pl.ds(at, STEP), columns(c)] = got[e * STEP : (e + 1) * STEP, :]
+
+        @pl.when(c + 2 < depth // width)
+        def _():
+            for copy in tokens(c + 2):
+                copy.start()
+
+    def put(j):
+        c = pl.ds(pl.multiple_of((j // late) * block, block), block)
+        at = lax.rem(j, 2)
+        return pltpu.make_async_copy(
+            piece.at[at], h_out.at[lax.rem(j, late), :, c], piece_sem.at[at]
+        )
+
+    @pl.loop(0, n_jobs)
+    def _(j):
+        e, slot = lax.rem(j, late), lax.rem(j, slots)
+        for copy in fetches(j):
+            copy.wait()
+        size = (begin(e, 4) + STEP - 1) // STEP
+
+        @pl.when(size == 0)
+        def _():
+            packed[...] = jnp.zeros_like(packed)
+
+        for v in range(1, 5):
+
+            @pl.when(size == v)
+            def _(v=v):
+                m = v * STEP
+                first = pl.multiple_of(e * 4 * STEP, 16)
+                both = dot(z[pl.ds(first, m), :], ring[slot])
+                packed[:m, :] = (silu(both[:, :block]) * both[:, block:]).astype(BF16)
+                packed[m : m + STEP, :] = jnp.zeros((STEP, block), BF16)
+
+        @pl.when(j + slots < n_jobs)
+        def _():
+            for copy in fetches(j + slots):
+                copy.start()
+
+        @pl.when(j >= 2)
+        def _():
+            put(j - 2).wait()
+
+        for k in range(4):
+            piece[lax.rem(j, 2), k * STEP : (k + 1) * STEP, :] = packed[pl.ds(begin(e, k), STEP), :]
+        put(j).start()
+
+    put(jnp.int32(n_jobs - 2)).wait()
+    put(jnp.int32(n_jobs - 1)).wait()
+
+
+def up(meta, code, x0, xs, w_gate, w_up, block):
     experts, depth, ff = w_gate.shape
     late = experts - EARLY
-    once = pl.Buffered(1)
-    weight = pl.BlockSpec((1, depth, block), lambda e, n, m: (e + EARLY, 0, n))
+    hbm, dma = pl.BlockSpec(memory_space=pl.ANY), pltpu.SemaphoreType.DMA
     return pl.pallas_call(
-        functools.partial(up_kernel, block),
-        grid_spec=pltpu.PrefetchScalarGridSpec(
-            num_scalar_prefetch=1,
-            grid=(late, ff // block),
-            in_specs=[
-                pl.BlockSpec((1, 4, 256), lambda e, n, m: (e + EARLY, 0, 0)),
-                pl.BlockSpec((256, depth), lambda e, n, m: (0, 0), pipeline_mode=once),
-                pl.BlockSpec((3, 256, depth), lambda e, n, m: (0, 0, 0), pipeline_mode=once),
-                weight,
-                weight,
-            ],
-            out_specs=pl.BlockSpec((1, 4 * STEP, block), lambda e, n, m: (e, 0, n)),
-            scratch_shapes=[
-                pltpu.VMEM((5 * STEP, depth), BF16),
-                pltpu.VMEM((5 * STEP, block), BF16),
-                pltpu.VMEM((4 * STEP, block), F32),
-            ],
-        ),
+        up_kernel,
+        in_specs=[
+            pl.BlockSpec(memory_space=pltpu.SMEM),
+            pl.BlockSpec(memory_space=pltpu.VMEM),
+            hbm, hbm, hbm, hbm,
+        ],
+        out_specs=hbm,
+        scratch_shapes=[
+            pltpu.VMEM(((4 * late + 1) * STEP, depth), BF16),
+            pltpu.VMEM((2, 4, 256, 1024), BF16),
+            pltpu.VMEM((3, depth, 2 * block), BF16),
+            pltpu.VMEM((5 * STEP, block), BF16),
+            pltpu.VMEM((2, 4 * STEP, block), BF16),
+            dma((2, 2)), dma((3, 2)), dma((2,)),
+        ],
         out_shape=jax.ShapeDtypeStruct((late, 4 * STEP, ff), BF16),
-        compiler_params=pltpu.CompilerParams(
-            vmem_limit_bytes=VMEM, dimension_semantics=("arbitrary", "arbitrary")
-        ),
+        compiler_params=pltpu.CompilerParams(vmem_limit_bytes=VMEM),
         cost_estimate=pl.CostEstimate(
             flops=late * 300 * depth * ff * 4,
             bytes_accessed=late * depth * ff * 4,
             transcendentals=0,
         ),
         name="up",
-    )(meta, code, x0, x1, w_gate, w_up)
+    )(meta, code, x0, xs, w_gate, w_up)
 
 
 def finish_kernel(
@@ -527,7 +590,7 @@
         starts.append(starts[-1] + used[:, k])
     meta = jnp.stack(starts + starts[:3], 1).reshape(-1)
 
-    late = up(meta, code, x, xs, w_gate, w_up, 512)
+    late = up(meta, code, x, xs, w_gate, w_up, 256)
     return finish(code, weight, early, late, w_down, shared, 512)[None, None]
 
 

time: 361 us -> 354 us (0.981); the launches traced: 366 us -> 353 us
  Pallas kernels: 356 us -> 343 us
    pallas_call x1, Pallas kernels: 141 us -> 121 us  [finish(): pl.pallas_call(functools.partial(finish_kernel, chunks), grid=(chunks + 3...]
    pallas_call x1, Pallas kernels: 107 us -> 114 us  [up(): pl.pallas_call(up_kernel, in_specs=[pl.BlockSpec(memory_space=pltpu.SMEM)...]
where the time goes in v5:
time: 354 us; the launch traced here: 353 us
  Pallas kernels  343 us (97%)
  local copies, waits for them, and re-layouts  4.79 us (1%)
  other arithmetic  4.59 us (1%)
    pallas_call x1, Pallas kernels, finish(): pl.pallas_call(functools.partial(finish_kernel, chunks), grid=(chunks + 3...  121 us
    pallas_call x1, Pallas kernels, up(): pl.pallas_call(up_kernel, in_specs=[pl.BlockSpec(memory_space=pltpu.SMEM)...  114 us
    pallas_call x1, Pallas kernels, arrive(): pl.pallas_call(functools.partial(arrive_kernel, local), in_specs=[vmem] *...  109 us

profile of v5, /device:TPU:0, one launch (start us, length us, event | category | flops | bytes accessed | tf_op | source)
XLA Modules:
  0.0 352.9 jit_solution(15871197585965048202)
XLA Ops:
  0.0 0.7 compare_bitcast_fusion
  0.7 0.7 add_bitcast_fusion
  1.4 0.8 select_reduce_fusion.1
  2.2 0.8 select_reduce_fusion
  3.0 0.6 pad_maximum_fusion.table
  3.6 108.8 %arrive.1 = (bf16[3,256,7168]{2,1,0:T(8,128)(2,1)}, f32[6,4,256]{2,1,0:T(4,128)}, f32[6,4,256]{2,1,0:T(4,128)}, bf16[2,448,2048]{2,1,0:T(8,128)(2,1)}, f32[256,7168]{1,0:T(8,128)}) custom-call(bf16[256,7168]{1,0:T(8,128)(2,1)} %bitcast.19, f32[2,24,256]{2,1,0:T(8,128)} %pad_maximum_fusion.table, bf16[6,7168,2048]{2,1,0:T(8,128)(2,1)} %w_gate.3, ...), custom_call_target="tpu_custom_call" | custom-call | tf_op jit(solution)/shard_map/arrive/pallas_call | solution.py:246
  112.5 0.8 reduce_max.9
  113.3 0.1 slice_add_fusion
  113.4 0.1 slice_add_fusion.1
  113.4 0.1 stack.16
  113.5 0.6 reshape.25.meta
  114.1 114.0 %up.1.late = bf16[4,448,2048]{2,1,0:T(8,128)(2,1)} custom-call(s32[48]{0:T(128)} %reshape.25.meta, f32[6,4,256]{2,1,0:T(4,128)} %get-tuple-element.10.code, bf16[256,7168]{1,0:T(8,128)(2,1)} %bitcast.20, bf16[3,256,7168]{2,1,0:T(8,128)(2,1)} %get-tuple-element.13.xs, bf16[6,7168,2048]{2,1,0:T(8,128)(2,1)} %w_gate.3, bf16[6,7168,2048]{2,1,0:T(8,128)(2,1)} %w_up.3), custom_call_target="tpu_custom_call" | custom-call | flops 70464307200 | bytes 234881024 | tf_op jit(solution)/shard_map/up/pallas_call | solution.py:393
  228.2 120.6 %finish.1 = bf16[256,7168]{1,0:T(8,128)(2,1)} custom-call(f32[6,4,256]{2,1,0:T(4,128)} %get-tuple-element.10.code, f32[6,4,256]{2,1,0:T(4,128)} %get-tuple-element.11.gate, bf16[2,448,2048]{2,1,0:T(8,128)(2,1)} %get-tuple-element.12.early, bf16[4,448,2048]{2,1,0:T(8,128)(2,1)} %up.1.late, bf16[6,2048,7168]{2,1,0:T(8,128)(2,1)} %wd.1, ...), custom_call_target="tpu_custom_call" | custom-call | tf_op jit(solution)/shard_map/finish/pallas_call | solution.py:540
  348.7 4.1 %copy.12 = bf16[1,1,256,7168]{3,2,1,0:T(8,128)(2,1)} copy(bf16[1,1,256,7168]{3,2,1,0:T(8,128)(2,1)} %bitcast.21) | data formatting | bytes 7340032
  (3 shorter events, 0.0 us)
